TPU v7x, 32 devices: a whole 2x2x4 slice. The times are simulated.
32 devices in a mesh: pod: 2 (over x), data: 4 (over z), model: 4 (over y, core).
Axes of the slice: x: 2, y: 2, z: 4, core: 2. Of those that a mesh axis runs over, the one named last changes fastest.
Arguments:
- x_in: bfloat16 [8, 1024, 2048], P(('pod', 'data'), 'model'), parts along dimension 0
- dy_in: bfloat16 [8, 1024, 2048], P(('pod', 'data'), 'model'), parts along dimension 0
- w_q: bfloat16 [2048, 16, 128], P(None, 'model')
- w_k: bfloat16 [2, 2048, 128], replicated
- w_v: bfloat16 [2, 2048, 128], replicated
- w_o: bfloat16 [16, 128, 2048], P('model')
Outputs:
- output 1: bfloat16 [8, 1024, 2048], P(('pod', 'data'), 'model'), parts along dimension 0
- output 2: float32 [4096, 16, 128], P(('pod', 'data'), 'model'), parts along dimension 0
- output 3: float32 [8192, 128], P(('pod', 'model', 'data')), parts along dimension 0
- output 4: float32 [8192, 128], P(('pod', 'model', 'data')), parts along dimension 0
- output 5: float32 [32, 128, 2048], P(('pod', 'model'), None, 'data'), parts along dimension 0
There are 2 independent parts. A program takes and returns all parts, laid end to end along the dimension named above; an argument that names none is the same for every part.
All inputs are finite; a program needn't handle non-finite values.
Results may differ from a plain program's by a relative error of at most 0.00935703.
Values are sent between devices in bfloat16 or wider.
A program may use at most 1 GiB of HBM per device.

v0:
```python
import jax
import jax.numpy as jnp
from jax import lax
from jax.sharding import PartitionSpec as P


def subgroup_pairs(step_shift, sub_size, axis_size):
    return [(start_dev + member, start_dev + (member + step_shift) % sub_size)
            for start_dev in range(0, axis_size, sub_size) for member in range(sub_size)]


def subgroup_scatter_sum(grad_parts, sub_size, axis_size):
    my_slot = lax.axis_index('model') % sub_size
    lead_dim, row_count, col_count = grad_parts.shape
    row_blocks = grad_parts.reshape(lead_dim, sub_size, row_count // sub_size, col_count)
    total_sum = lax.dynamic_index_in_dim(row_blocks, my_slot, axis=1, keepdims=False)
    for step_shift in range(1, sub_size):
        outgoing = lax.dynamic_index_in_dim(row_blocks, (my_slot + step_shift) % sub_size, axis=1, keepdims=False)
        total_sum = total_sum + lax.ppermute(outgoing, 'model', subgroup_pairs(step_shift, sub_size, axis_size))
    return total_sum


def solution(mesh):
    model_size = mesh.shape['model']
    tok_spec = P(('pod', 'data'), 'model', None)

    def device_step(x_loc, dy_loc, w_q, w_k, w_v, w_o):
        kv_heads = w_k.shape[0]
        head_dim = w_k.shape[2]
        sub_size = model_size // kv_heads
        score_scale = head_dim ** -0.5
        kv_index = lax.axis_index('model') // sub_size
        x_full = lax.all_gather(x_loc, 'model', axis=1, tiled=True)
        dy_full = lax.all_gather(dy_loc, 'model', axis=1, tiled=True)
        kv_weights = jnp.stack([lax.dynamic_index_in_dim(w_k, kv_index, axis=0, keepdims=False),
                                lax.dynamic_index_in_dim(w_v, kv_index, axis=0, keepdims=False)])
        seq_len = x_full.shape[1]
        causal = lax.broadcasted_iota(jnp.int32, (seq_len, seq_len), 0) >= lax.broadcasted_iota(jnp.int32, (seq_len, seq_len), 1)
        q_loc = jnp.einsum('btd,dhe->bhte', x_full, w_q, preferred_element_type=jnp.float32).astype(jnp.bfloat16)
        kv_loc = jnp.einsum('btd,nde->nbte', x_full, kv_weights, preferred_element_type=jnp.float32).astype(jnp.bfloat16)
        k_loc = kv_loc[0]
        v_loc = kv_loc[1]
        scores = jnp.einsum('bhqe,bke->bhqk', q_loc, k_loc, preferred_element_type=jnp.float32) * score_scale
        attn_prob = jax.nn.softmax(jnp.where(causal, scores, -jnp.inf), axis=-1)
        prob_bf = attn_prob.astype(jnp.bfloat16)
        out_loc = jnp.einsum('bhqk,bke->bhqe', prob_bf, v_loc, preferred_element_type=jnp.float32).astype(jnp.bfloat16)
        dout_loc = jnp.einsum('btd,hed->bhte', dy_full, w_o, preferred_element_type=jnp.float32).astype(jnp.bfloat16)
        grad_prob = jnp.einsum('bhqe,bke->bhqk', dout_loc, v_loc, preferred_element_type=jnp.float32)
        row_delta = jnp.einsum('bhqe,bhqe->bhq', dout_loc, out_loc, preferred_element_type=jnp.float32)
        grad_score = (attn_prob * (grad_prob - row_delta[..., None])).astype(jnp.bfloat16)
        grad_q = (jnp.einsum('bhqk,bke->bhqe', grad_score, k_loc, preferred_element_type=jnp.float32) * score_scale).astype(jnp.bfloat16)
        grad_k = jnp.einsum('bhqk,bhqe->bke', grad_score, q_loc, preferred_element_type=jnp.float32) * score_scale
        grad_v = jnp.einsum('bhqk,bhqe->bke', prob_bf, dout_loc, preferred_element_type=jnp.float32)
        grad_kv = jnp.stack([grad_k, grad_v]).astype(jnp.bfloat16)
        dx_part = (jnp.einsum('bhte,dhe->btd', grad_q, w_q, preferred_element_type=jnp.float32)
                   + jnp.einsum('nbte,nde->btd', grad_kv, kv_weights, preferred_element_type=jnp.float32))
        dwq_part = jnp.einsum('btd,bhte->dhe', x_full, grad_q, preferred_element_type=jnp.float32)
        dwkv_part = jnp.einsum('btd,nbte->nde', x_full, grad_kv, preferred_element_type=jnp.float32)
        dwo_part = jnp.einsum('bhte,btd->hed', out_loc, dy_full, preferred_element_type=jnp.float32)
        dx_loc = lax.psum_scatter(dx_part, 'model', scatter_dimension=1, tiled=True).astype(jnp.bfloat16)
        dwkv_sub = subgroup_scatter_sum(dwkv_part, sub_size, model_size)
        dwkv_loc = lax.psum_scatter(dwkv_sub, 'data', scatter_dimension=1, tiled=True)
        dwq_loc = lax.psum_scatter(dwq_part, 'data', scatter_dimension=0, tiled=True)
        dwo_loc = lax.psum_scatter(dwo_part, 'data', scatter_dimension=2, tiled=True)
        return dx_loc, dwq_loc, dwkv_loc[0], dwkv_loc[1], dwo_loc

    kv_rows = P(('pod', 'model', 'data'), None)
    return jax.shard_map(device_step, mesh=mesh,
                         in_specs=(tok_spec, tok_spec, P(None, 'model', None), P(), P(), P('model', None, None)),
                         out_specs=(tok_spec, P(('pod', 'data'), 'model', None), kv_rows, kv_rows, P(('pod', 'model'), None, 'data')),
                         check_vma=False)
```

profile of v0, /device:TPU:0, one launch (start us, length us, event | category | flops | bytes accessed | tf_op | source)
XLA Modules:
  0.0 411.6 jit_solution(14235232477053984852)
XLA Ops:
  7.2 0.0 all-gather.5.cloned.1.call-start
  7.2 0.7 all-gather.5.cloned.1.call-update
  7.9 0.0 all-gather.3.cloned.1.call-start
  8.0 0.7 all-gather.3.cloned.1.call-update
  8.7 0.0 reduce-scatter.9.cloned.1.call-start
  8.8 2.1 constant_dynamic-slice_fusion.2
  10.8 0.2 copy.57
  11.0 1.4 copy.56
  12.5 1.3 iota_compare_fusion
  13.8 32.8 %all-gather.5.cloned.1.call-done = bf16[1,1024,2048]{2,1,0:T(8,128)(2,1)} async-done(((bf16[1,256,2048]{2,1,0:T(8,128)(2,1)}), bf16[1,1024,2048]{2,1,0:T(8,128)(2,1)}) %all-gather.5.cloned.1.call-update) | async-done | bytes 4194320 | tf_op jit(solution)/shard_map/all_gather | solution.py:34
  46.6 5.5 %fusion.38 = bf16[4,1024,128]{1,2,0:T(8,128)(2,1)} fusion(bf16[4,128,2048]{2,1,0:T(8,128)(2,1)S(1)} %copy-done, bf16[1,1024,2048]{2,1,0:T(8,128)(2,1)} %all-gather.5.cloned.1.call-done), kind=kOutput, calls=%fused_computation.36 | convolution fusion | flops 2148007936 | bytes 7340032 | tf_op jit(solution)/shard_map/btd,hed->bhte/dot_general | solution.py:47
  52.2 1.5 copy.43
  53.6 28.9 %all-gather.3.cloned.1.call-done = bf16[1,1024,2048]{2,1,0:T(8,128)(2,1)} async-done(((bf16[1,256,2048]{2,1,0:T(8,128)(2,1)}), bf16[1,1024,2048]{2,1,0:T(8,128)(2,1)}) %all-gather.3.cloned.1.call-update) | async-done | bytes 4194320 | tf_op jit(solution)/shard_map/all_gather | solution.py:33
  82.5 6.3 %fusion.41 = bf16[4,1024,128]{1,2,0:T(8,128)(2,1)} fusion(bf16[1,1024,2048]{2,1,0:T(8,128)(2,1)} %all-gather.3.cloned.1.call-done, bf16[2048,4,128]{2,1,0:T(4,128)(2,1)} %param.8), kind=kOutput, calls=%fused_computation.37 | convolution fusion | flops 2148007936 | bytes 7340032 | tf_op jit(solution)/shard_map/btd,dhe->bhte/dot_general | solution.py:39
  88.8 2.2 fusion.49
  91.1 10.6 %fusion.63 = (f32[4,1024]{1,0:T(4,128)S(1)}, f32[4,1024,1024]{1,2,0:T(8,128)}) fusion(pred[1024,1024]{0,1:T(8,128)(4,1)} %iota_compare_fusion, bf16[4,1024,128]{1,2,0:T(8,128)(2,1)} %fusion.41, bf16[2,1,1024,128]{2,3,0,1:T(8,128)(2,1)} %fusion.49), kind=kOutput, calls=%fused_computation.64 | convolution fusion | flops 1090520064 | bytes 19152896 | tf_op jit(solution)/shard_map/sub | solution.py:44
  101.6 7.2 %fusion.6 = bf16[4,1024,1024]{1,2,0:T(8,128)(2,1)S(1)} fusion(f32[4,1024,1024]{1,2,0:T(8,128)} %get-tuple-element.15, f32[4,1024]{1,0:T(4,128)S(1)} %get-tuple-element.14), kind=kLoop, calls=%fused_computation.11 | loop fusion | flops 8388608 | bytes 25182208 | tf_op jit(solution)/shard_map/convert_element_type | solution.py:45
  108.9 2.3 fusion.55
  111.2 2.8 multiply_reduce_fusion
  114.0 9.9 %multiply_convert_fusion = bf16[4,1024,1024]{1,2,0:T(8,128)(2,1)} fusion(bf16[4,1024,128]{1,2,0:T(8,128)(2,1)S(1)} %copy-done.11, f32[4,1024]{1,0:T(4,128)S(1)} %get-tuple-element.16, f32[4,1024,1024]{1,2,0:T(8,128)} %get-tuple-element.15, f32[4,1024]{1,0:T(4,128)S(1)} %get-tuple-element.14, bf16[2,1,1024,128]{2,3,0,1:T(8,128)(2,1)S(1)} %copy-done.12), kind=kOutput, calls=%fused_computation.1 | convolution fusion | flops 1090519040 | bytes 26509312 | tf_op jit(solution)/shard_map/bhqe,bke->bhqk/dot_general | solution.py:48
  123.9 5.9 %fusion.56 = bf16[1,1024,128]{2,1,0:T(8,128)(2,1)S(1)} fusion(bf16[4,1024,1024]{1,2,0:T(8,128)(2,1)} %multiply_convert_fusion, bf16[4,1024,128]{1,2,0:T(8,128)(2,1)S(1)} %copy-done.13), kind=kOutput, calls=%fused_computation.46 | convolution fusion | flops 1074003968 | bytes 9699328 | tf_op jit(solution)/shard_map/bhqk,bhqe->bke/dot_general | solution.py:52
  129.8 0.7 copy-done.9
  130.5 2.6 fusion.22
  133.1 3.2 reshape.132
  136.4 3.1 constant_dynamic-slice_fusion.1
  139.5 3.6 copy.30
  143.1 0.2 collective-permute-start
  143.3 2.3 copy.29
  145.7 0.1 collective-permute-done
  145.8 1.1 bitcast_add_fusion.1
  146.8 0.0 reduce-scatter.9.cloned.1.call-update
  146.9 0.0 reduce-scatter.7.cloned.1.call-start
  146.9 5.9 %multiply_convert_fusion.1 = bf16[4,1024,128]{2,1,0:T(8,128)(2,1)S(1)} fusion(bf16[4,1024,1024]{1,2,0:T(8,128)(2,1)} %multiply_convert_fusion, bf16[2,1,1024,128]{2,3,0,1:T(8,128)(2,1)} %fusion.49), kind=kOutput, calls=%fused_computation.28 | convolution fusion | flops 1074790400 | bytes 9699328 | tf_op jit(solution)/shard_map/bhqk,bke->bhqe/dot_general | solution.py:51
  152.9 4.4 %fusion.19 = f32[2048,4,128]{0,2,1:T(8,128)} fusion(bf16[4,1024,128]{2,1,0:T(8,128)(2,1)S(1)} %multiply_convert_fusion.1, bf16[1,1024,2048]{2,1,0:T(8,128)(2,1)S(1)} %copy-done.4), kind=kOutput, calls=%fused_computation.25 | convolution fusion | flops 2147483648 | bytes 9437184 | tf_op jit(solution)/shard_map/btd,bhte->dhe/dot_general | solution.py:57
  157.3 0.0 reduce-scatter.7.cloned.1.call-update
  157.3 0.0 reduce-scatter.5.cloned.1.call-start
  157.4 4.1 fusion.26
  161.5 4.5 %fusion.2 = f32[1,1024,2048]{2,1,0:T(8,128)} fusion(f32[1024,2048,1]{1,0,2:T(8,128)S(1)} %fusion.26, bf16[1,2048,128]{1,2,0:T(8,128)(2,1)S(1)} %copy-done.6, bf16[1,2048,128]{1,2,0:T(8,128)(2,1)S(1)} %copy-done.8, bf16[1,1024,128]{2,1,0:T(8,128)(2,1)S(1)} %fusion.55, bf16[1,1024,128]{2,1,0:T(8,128)(2,1)S(1)} %copy-done.10), kind=kOutput, calls=%fused_computation.6 | convolution fusion | flops 1076625408 | bytes 18350080 | tf_op jit(solution)/shard_map/nbte,nde->btd/dot_general | solution.py:56
  166.0 0.3 reduce-scatter.11.cloned.1.call-start
  166.3 6.5 %fusion.7 = f32[4,128,2048]{2,1,0:T(8,128)} fusion(bf16[4,1024,128]{2,1,0:T(8,128)(2,1)S(1)} %get-tuple-element.17, bf16[1,1024,2048]{2,1,0:T(8,128)(2,1)} %all-gather.5.cloned.1.call-done), kind=kOutput, calls=%fused_computation.12 | convolution fusion | flops 2147483648 | bytes 9437184 | tf_op jit(solution)/shard_map/bhte,btd->hed/dot_general | solution.py:59
  172.9 0.0 reduce-scatter.11.cloned.1.call-update
  172.9 1.4 reduce-scatter.9.cloned.1.call-done
  174.3 1.7 slice_bitcast_fusion.11
  176.0 75.6 %reduce-scatter.7.cloned.1.call-done = f32[512,4,128]{0,2,1:T(8,128)} async-done(((f32[2048,4,128]{0,2,1:T(8,128)}), f32[512,4,128]{0,2,1:T(8,128)}) %reduce-scatter.7.cloned.1.call-update) | async-done | bytes 1048592 | tf_op jit(solution)/shard_map/reduce_scatter | solution.py:63
  251.6 2.5 copy.32
  254.2 71.1 %reduce-scatter.5.cloned.1.call-done = f32[1,256,2048]{2,1,0:T(8,128)} async-done(((f32[1,1024,2048]{2,1,0:T(8,128)}), f32[1,256,2048]{2,1,0:T(8,128)}) %reduce-scatter.5.cloned.1.call-update) | async-done | bytes 2097168 | tf_op jit(solution)/shard_map/reduce_scatter | solution.py:60
  325.3 2.7 convert_element_type.64
  328.0 76.7 %reduce-scatter.11.cloned.1.call-done = f32[4,128,512]{2,1,0:T(8,128)} async-done(((f32[4,128,2048]{2,1,0:T(8,128)}), f32[4,128,512]{2,1,0:T(8,128)}) %reduce-scatter.11.cloned.1.call-update) | async-done | bytes 1048592 | tf_op jit(solution)/shard_map/reduce_scatter | solution.py:64
  (28 shorter events, 0.1 us)
Async XLA Ops:
  7.2 39.5 %copy-start = (bf16[4,128,2048]{2,1,0:T(8,128)(2,1)S(1)}, bf16[4,128,2048]{2,1,0:T(8,128)(2,1)}, u32[]{:S(2)}) copy-start(bf16[4,128,2048]{2,1,0:T(8,128)(2,1)} %param.11) | copy-start | bytes 6291460
  7.2 39.4 %all-gather.5.cloned.1.call-start = ((), (), s32[]{:S(2)}) async-start(), calls=%async_computation.5 | async-start | bytes 5242880 | tf_op jit(solution)/shard_map/all_gather | solution.py:34
  7.9 74.6 %all-gather.3.cloned.1.call-start = ((), (), s32[]{:S(2)}) async-start(), calls=%async_computation.4 | async-start | bytes 5242880 | tf_op jit(solution)/shard_map/all_gather | solution.py:33
  8.7 165.7 %reduce-scatter.9.cloned.1.call-start = ((), (), s32[]{:S(2)}) async-start(), calls=%async_computation.8 | async-start | bytes 1310720 | tf_op jit(solution)/shard_map/reduce_scatter | solution.py:62
  11.0 77.8 %copy-start.5 = (bf16[1,2048,128]{1,2,0:T(8,128)(2,1)}, bf16[1,2048,128]{1,2,0:T(8,128)(2,1)S(1)}, u32[]{:S(2)}) copy-start(bf16[1,2048,128]{1,2,0:T(8,128)(2,1)S(1)} %copy.57) | copy-start | bytes 1572868
  12.5 76.3 %copy-start.7 = (bf16[1,2048,128]{1,2,0:T(8,128)(2,1)}, bf16[1,2048,128]{1,2,0:T(8,128)(2,1)S(1)}, u32[]{:S(2)}) copy-start(bf16[1,2048,128]{1,2,0:T(8,128)(2,1)S(1)} %copy.56) | copy-start | bytes 1572868
  82.5 6.3 %copy-start.2 = (bf16[1,1024,2048]{2,1,0:T(8,128)(2,1)S(1)}, bf16[1,1024,2048]{2,1,0:T(8,128)(2,1)}, u32[]{:S(2)}) copy-start(bf16[1,1024,2048]{2,1,0:T(8,128)(2,1)} %all-gather.3.cloned.1.call-done) | copy-start | bytes 12582916
  101.6 7.2 %copy-start.11 = (bf16[4,1024,128]{1,2,0:T(8,128)(2,1)S(1)}, bf16[4,1024,128]{1,2,0:T(8,128)(2,1)}, u32[]{:S(2)}) copy-start(bf16[4,1024,128]{1,2,0:T(8,128)(2,1)} %fusion.38) | copy-start | bytes 3145732
  108.8 2.4 copy-start.12
  114.0 9.9 %copy-start.13 = (bf16[4,1024,128]{1,2,0:T(8,128)(2,1)S(1)}, bf16[4,1024,128]{1,2,0:T(8,128)(2,1)}, u32[]{:S(2)}) copy-start(bf16[4,1024,128]{1,2,0:T(8,128)(2,1)} %fusion.41) | copy-start | bytes 3145732
  123.9 6.6 %copy-start.3 = (bf16[1,1024,2048]{2,1,0:T(8,128)(2,1)S(1)}, bf16[1,1024,2048]{2,1,0:T(8,128)(2,1)}, u32[]{:S(2)}) copy-start(bf16[1,1024,2048]{2,1,0:T(8,128)(2,1)} %all-gather.3.cloned.1.call-done) | copy-start | bytes 12582916
  129.8 0.7 copy-start.9
  143.1 2.7 collective-permute-start
  146.9 104.8 %reduce-scatter.7.cloned.1.call-start = ((), (), s32[]{:S(2)}) async-start(), calls=%async_computation.7 | async-start | bytes 5242880 | tf_op jit(solution)/shard_map/reduce_scatter | solution.py:63
  146.9 6.0 %copy-start.4 = (bf16[1,1024,2048]{2,1,0:T(8,128)(2,1)S(1)}, bf16[1,1024,2048]{2,1,0:T(8,128)(2,1)}, u32[]{:S(2)}) copy-start(bf16[1,1024,2048]{2,1,0:T(8,128)(2,1)} %all-gather.3.cloned.1.call-done) | copy-start | bytes 12582916
  157.3 4.1 %copy-start.6 = (bf16[1,2048,128]{1,2,0:T(8,128)(2,1)S(1)}, bf16[1,2048,128]{1,2,0:T(8,128)(2,1)}, u32[]{:S(2)}) copy-start(bf16[1,2048,128]{1,2,0:T(8,128)(2,1)} %copy-done.5) | copy-start | bytes 1572868
  157.3 4.1 %copy-start.8 = (bf16[1,2048,128]{1,2,0:T(8,128)(2,1)S(1)}, bf16[1,2048,128]{1,2,0:T(8,128)(2,1)}, u32[]{:S(2)}) copy-start(bf16[1,2048,128]{1,2,0:T(8,128)(2,1)} %copy-done.7) | copy-start | bytes 1572868
  157.3 167.9 %reduce-scatter.5.cloned.1.call-start = ((), (), s32[]{:S(2)}) async-start(), calls=%async_computation.6 | async-start | bytes 10485760 | tf_op jit(solution)/shard_map/reduce_scatter | solution.py:60
  157.4 4.1 copy-start.10
  166.0 238.7 %reduce-scatter.11.cloned.1.call-start = ((), (), s32[]{:S(2)}) async-start(), calls=%async_computation.9 | async-start | bytes 5242880 | tf_op jit(solution)/shard_map/reduce_scatter | solution.py:64
  172.8 231.9 %copy-start.1 = (bf16[4,128,2048]{2,1,0:T(8,128)(2,1)S(1)}, bf16[4,128,2048]{2,1,0:T(8,128)(2,1)}, u32[]{:S(2)}) copy-start(bf16[4,128,2048]{2,1,0:T(8,128)(2,1)} %param.11) | copy-start | bytes 6291460
Sparse Core Ops, SparseCore 0:
  9.6 37.0 all-gather.4
  48.2 34.2 all-gather.2
  147.0 27.2 reduce-scatter.8
  176.5 75.1 reduce-scatter.6
  254.1 71.1 reduce-scatter.4
  328.0 76.6 reduce-scatter.10
where the time goes:
time: 412 us
  waiting for transfers between devices  288 us (70%)
  matrix products  73.6 us (18%)
  local copies, waits for them, and re-layouts  22.5 us (5%)
  between operations  14.4 us (3%)
  other arithmetic  12.3 us (3%)
    reduce_scatter x1, waiting for transfers between devices, device_step(): lax.psum_scatter(dwo_part, 'data', scatter_dimension=2, tiled=True)  76.7 us
    reduce_scatter x1, waiting for transfers between devices, device_step(): lax.psum_scatter(dwq_part, 'data', scatter_dimension=0, tiled=True)  75.6 us
    reduce_scatter x1, waiting for transfers between devices, device_step(): lax.psum_scatter(dx_part, 'model', scatter_dimension=1, tiled=True)  71.1 us
    all_gather x1, waiting for transfers between devices, device_step(): dy_full = lax.all_gather(dy_loc, 'model', axis=1, tiled=True)  32.8 us
    all_gather x1, waiting for transfers between devices, device_step(): x_full = lax.all_gather(x_loc, 'model', axis=1, tiled=True)  28.9 us
    sub x1, matrix products, device_step(): attn_prob = jax.nn.softmax(jnp.where(causal, scores, -jnp.inf), axis=-1)  10.6 us
    dot_general x1, matrix products, device_step(): jnp.einsum('bhqe,bke->bhqk', dout_loc, v_loc, preferred_element_type=jnp....  9.86 us
  transfers between devices with their start and end apart: 7, of which 7 were waited for; matrix products, arithmetic and copies ran while one was open for 11% of the time, Pallas kernels for 0%

commit v1 on v0

v1 whole, which is shorter than its diff:
```python
import functools
import math

import jax
import jax.numpy as jnp
from jax import lax
from jax.experimental import pallas as pl
from jax.experimental.pallas import tpu as pltpu
from jax.sharding import PartitionSpec as P

MESH = pl.DeviceIdType.MESH
F32 = jnp.float32
BF16 = jnp.bfloat16

SEQ = 1024
BLK = 256
DIM = 2048
HD = 128
NH = 4
HE = NH * HD
QKV = HE + 2 * HD
CH = 512
KC = 256
NX = 2
XR = BLK // NX
NB = SEQ // BLK
CAUSAL_ROWS = BLK * NB * (NB + 1) // 2

S_XY, S_XF, S_XC = 0, 2, 4
S_DY, S_DF, S_DC = 5, 9, 13
S_WO, S_WQ = 14, 26
S_KV = 38
S_KP = 41
S_PX = 42
S_PY = 44
N_SEM = 46


def nn(a, b):
    return lax.dot_general(a, b, (((1,), (0,)), ((), ())), preferred_element_type=F32)


def nt(a, b):
    return lax.dot_general(a, b, (((1,), (1,)), ((), ())), preferred_element_type=F32)


def step_kernel(x_in, dy_in, wq_in, wk_in, wv_in, wo_in, dx_out, dwq_out, dwkv_out, dwo_out,
                xg, dyg, wqkv, wo, qkv, kt, vt, prob, pbuf, ot, dout, at, am, dkv, pw, pq, pkv,
                kvs, kvr, sring, rring, skv, rkv, sx, rx, sy, ry, pxo, pxm, dxo, ssem, rsem, lsem):
    pod = lax.axis_index("pod")
    z = lax.axis_index("data")
    m = lax.axis_index("model")
    y = m // 2
    c = m % 2
    core_m = 2 * y + 1 - c
    far_m = (m + 2) % 4
    diag_m = (core_m + 2) % 4
    core_dev = (pod, z, core_m)
    far_dev = (pod, z, far_m)
    right_dev = (pod, (z + 1) % 4, m)
    left_dev = (pod, (z + 3) % 4, m)

    def rows(block, n=BLK, off=0):
        return pl.ds(pl.multiple_of(block * BLK + off, n), n)

    def col(i):
        return pl.ds(pl.multiple_of(((z + 3 - i) % 4) * CH, CH), CH)

    def remote(src, dst, sem, dev):
        return pltpu.make_async_remote_copy(src_ref=src, dst_ref=dst, send_sem=ssem.at[sem], recv_sem=rsem.at[sem],
                                            device_id=dev, device_id_type=MESH)

    def head_rows(h):
        return pl.ds(pl.multiple_of(h * HD, HD), HD)

    loads = [
        pltpu.make_async_copy(x_in.at[0], xg.at[rows(m)], lsem.at[0]),
        pltpu.make_async_copy(dy_in.at[0], dyg.at[rows(m)], lsem.at[1]),
        pltpu.make_async_copy(wk_in.at[y], wqkv.at[:, pl.ds(HE, HD)], lsem.at[2]),
        pltpu.make_async_copy(wv_in.at[y], wqkv.at[:, pl.ds(HE + HD, HD)], lsem.at[3]),
        pltpu.make_async_copy(wq_in, wqkv.at[:, pl.ds(0, HE)], lsem.at[4]),
        pltpu.make_async_copy(wo_in, wo, lsem.at[5]),
    ]
    for ld in loads:
        ld.start()

    barrier = pltpu.get_barrier_semaphore()
    for dev in (far_dev, core_dev, right_dev, left_dev):
        pl.semaphore_signal(barrier, inc=1, device_id=dev, device_id_type=MESH)
    pl.semaphore_wait(barrier, 4)

    def x_far(i, block):
        r = rows(block, XR, i * XR)
        return remote(xg.at[r], xg.at[r], S_XY + i, far_dev)

    def x_fwd(i, block):
        r = rows(block, XR, i * XR)
        return remote(xg.at[r], xg.at[r], S_XF + i, core_dev)

    def x_core(block):
        return remote(xg.at[rows(block)], xg.at[rows(block)], S_XC, core_dev)

    def dy_far(i, block):
        return remote(dyg.at[rows(block), col(i)], dyg.at[rows(block), col(i)], S_DY + i, far_dev)

    def dy_fwd(i, block):
        return remote(dyg.at[rows(block), col(i)], dyg.at[rows(block), col(i)], S_DF + i, core_dev)

    def dy_core(block):
        return remote(dyg.at[rows(block)], dyg.at[rows(block)], S_DC, core_dev)

    loads[0].wait()
    for i in range(NX):
        x_far(i, m).start()
    x_core(m).start()
    loads[1].wait()
    for i in range(4):
        dy_far(i, m).start()
    dy_core(m).start()
    for ld in loads[2:]:
        ld.wait()

    def project(r):
        qkv[r, :] = nn(xg[r, :], wqkv[...]).astype(BF16)

    project(rows(m))
    x_core(core_m).wait_recv()
    project(rows(core_m))

    def x_piece(i, carry):
        x_far(i, far_m).wait_recv()
        x_fwd(i, far_m).start()
        project(rows(far_m, XR, i * XR))
        x_fwd(i, diag_m).wait_recv()
        project(rows(diag_m, XR, i * XR))
        return carry

    lax.fori_loop(0, NX, x_piece, 0)

    kt[...] = qkv[:, pl.ds(HE, HD)].T
    vt[...] = qkv[:, pl.ds(HE + HD, HD)].T
    dy_core(core_m).wait_recv()

    def take_dy(i):
        dy_far(i, far_m).wait_recv()
        dy_fwd(i, far_m).start()

    def ring_copy(base, which, hop, h):
        return remote(sring.at[which, hop, h], rring.at[which, hop, h], base + hop * 4 + h, right_dev)

    scale = HD ** -0.5
    exp_scale = scale * math.log2(math.e)
    diag_mask = lax.broadcasted_iota(jnp.int32, (BLK, BLK), 0) <= lax.broadcasted_iota(jnp.int32, (BLK, BLK), 1)

    def prow(qi, kj):
        return pl.ds(BLK * (qi * (qi + 1) // 2 + kj), BLK)

    def fwd_head(h, carry):
        hr = head_rows(h)
        for qi in range(NB):
            qb = qkv[pl.ds(qi * BLK, BLK), hr]
            mx = None
            for kj in range(qi + 1):
                s = nt(qkv[pl.ds(kj * BLK, BLK), pl.ds(HE, HD)], qb)
                if kj == qi:
                    s = jnp.where(diag_mask, s, -jnp.inf)
                prob[h, prow(qi, kj), :] = s
                bm = jnp.max(s, axis=0, keepdims=True)
                mx = bm if mx is None else jnp.maximum(mx, bm)
            tot = None
            for kj in range(qi + 1):
                e = jnp.exp2((prob[h, prow(qi, kj), :] - mx) * exp_scale)
                prob[h, prow(qi, kj), :] = e
                bs = jnp.sum(e, axis=0, keepdims=True)
                tot = bs if tot is None else tot + bs
            inv = 1.0 / tot
            for kj in range(qi + 1):
                p = prob[h, prow(qi, kj), :] * inv
                prob[h, prow(qi, kj), :] = p
                pbuf[pl.ds(kj * BLK, BLK), :] = p.astype(BF16)
            n = (qi + 1) * BLK
            ot[hr, pl.ds(qi * BLK, BLK)] = nn(vt[:, pl.ds(0, n)], pbuf[pl.ds(0, n), :]).astype(BF16)

        @pl.when(h == 0)
        def _():
            take_dy(0)
            dy_fwd(0, diag_m).wait_recv()

        sring[0, 0, h] = nn(ot[hr, :], dyg[:, col(0)]).astype(BF16)
        ring_copy(S_WO, 0, 0, h).start()
        return carry

    lax.fori_loop(0, NH, fwd_head, 0)

    def ring_service(base, which, own, hop, h):
        ring_copy(base, which, hop - 1, h).wait_recv()
        total = own[hop - 1, head_rows(h), :] + rring[which, hop - 1, h].astype(F32)
        sring[which, hop, h] = total.astype(BF16)
        ring_copy(base, which, hop, h).start()

    def ring_final(base, which, own, h):
        ring_copy(base, which, 2, h).wait_recv()
        own[2, head_rows(h), :] = own[2, head_rows(h), :] + rring[which, 2, h].astype(F32)

    def wo_own(i):
        pw[i - 1] = nn(ot[...], dyg[:, col(i)])

    def wq_own(i):
        pq[i - 1] = nn(at[pl.ds(0, HE), :], xg[:, col(i)])

    for i in range(1, 4):
        take_dy(i)
        dy_fwd(i, diag_m).wait_recv()
        wo_own(i)
        if i < 3:
            for h in range(2):
                ring_service(S_WO, 0, pw, 1, 2 * (i - 1) + h)

    def dout_block(b, carry):
        r = rows(b)
        dout[r, :] = nt(dyg[r, :], wo[...]).astype(BF16)
        return carry

    lax.fori_loop(0, NB, dout_block, 0)
    for h in range(2):
        ring_service(S_WO, 0, pw, 2, h)

    dkv[...] = jnp.zeros_like(dkv)

    def bwd_head(h, carry):
        hr = head_rows(h)
        for qi in range(NB):
            qr = pl.ds(qi * BLK, BLK)
            dob = dout[qr, hr]
            qb = qkv[qr, hr]
            delta = jnp.sum(dob.astype(F32).T * ot[hr, qr].astype(F32), axis=0, keepdims=True)
            for kj in range(qi + 1):
                kr = pl.ds(kj * BLK, BLK)
                p = prob[h, prow(qi, kj), :]
                dp = nt(qkv[kr, pl.ds(HE + HD, HD)], dob)
                ds = (p * (dp - delta)).astype(BF16)
                pbuf[kr, :] = ds
                dkv[kr, pl.ds(0, HD)] += nn(ds, qb)
                dkv[kr, pl.ds(HD, HD)] += nn(p.astype(BF16), dob)
            n = (qi + 1) * BLK
            dq = (nn(kt[:, pl.ds(0, n)], pbuf[pl.ds(0, n), :]) * scale).astype(BF16)
            at[hr, qr] = dq
            am[qr, hr] = dq.T

        @pl.when(h < 2)
        def _():
            ring_service(S_WO, 0, pw, 2, h + 2)

        sring[1, 0, h] = nn(at[hr, :], xg[:, col(0)]).astype(BF16)
        ring_copy(S_WQ, 1, 0, h).start()
        return carry

    lax.fori_loop(0, NH, bwd_head, 0)

    dkb = (dkv[:, pl.ds(0, HD)] * scale).astype(BF16)
    dvb = dkv[:, pl.ds(HD, HD)].astype(BF16)
    am[:, pl.ds(HE, HD)] = dkb
    am[:, pl.ds(HE + HD, HD)] = dvb
    at[pl.ds(HE, HD), :] = dkb.T
    at[pl.ds(HE + HD, HD), :] = dvb.T

    def dx_part(block, put):
        def piece(i, carry):
            cs = pl.ds(pl.multiple_of(i * CH, CH), CH)
            put(cs, nt(am[rows(block), :], wqkv[cs, :]))
            return carry

        lax.fori_loop(0, DIM // CH, piece, 0)

    def px_copy(i):
        return remote(sx.at[i], rx.at[i], S_PX + i, core_dev)

    def py_copy(i):
        r = pl.ds(i * (BLK // 2), BLK // 2)
        return remote(sy.at[r], ry.at[r], S_PY + i, far_dev)

    def put_sx(i):
        def put(cs, v):
            sx[i, :, cs] = v.astype(BF16)
        return put

    def put_ref(ref):
        def put(cs, v):
            ref[:, cs] = v
        return put

    dx_part(diag_m, put_sx(0))
    px_copy(0).start()
    dx_part(far_m, put_ref(pxm))
    px_copy(0).wait_recv()
    for i in range(2):
        r = pl.ds(i * (BLK // 2), BLK // 2)
        sy[r, :] = (pxm[r, :] + rx[0, r, :].astype(F32)).astype(BF16)
        py_copy(i).start()

    wq_own(1)
    for h in range(2):
        ring_service(S_WQ, 1, pq, 1, h)

    atk = at[pl.ds(HE, 2 * HD), :]
    half = DIM // 2
    kvs[...] = nn(atk, xg[:, pl.ds(pl.multiple_of((1 - c) * half, half), half)]).astype(BF16)
    kp_copy = remote(kvs, kvr, S_KP, core_dev)
    kp_copy.start()
    for h in range(2, 4):
        ring_service(S_WQ, 1, pq, 1, h)
    pkv[...] = nn(atk, xg[:, pl.ds(pl.multiple_of(c * half, half), half)])
    kp_copy.wait_recv()
    pkv[...] += kvr[...].astype(F32)

    def kcol(i):
        return pl.ds(pl.multiple_of(((z + 3 - i) % 4) * KC, KC), KC)

    def kv_copy(hop):
        return remote(skv.at[hop], rkv.at[hop], S_KV + hop, right_dev)

    skv[0] = pkv[:, kcol(0)].astype(BF16)
    kv_copy(0).start()

    wq_own(2)
    for h in range(2):
        ring_service(S_WQ, 1, pq, 2, h)
    dx_part(core_m, put_sx(1))
    px_copy(1).start()
    for h in range(2, 4):
        ring_service(S_WQ, 1, pq, 2, h)

    def kv_service(hop):
        kv_copy(hop - 1).wait_recv()
        skv[hop] = (pkv[:, kcol(hop)] + rkv[hop - 1].astype(F32)).astype(BF16)
        kv_copy(hop).start()

    kv_service(1)
    wq_own(3)
    dx_part(m, put_ref(pxo))
    px_copy(1).wait_recv()
    pxo[...] += rx[1].astype(F32)

    def wo_fin(h, carry):
        ring_final(S_WO, 0, pw, h)
        return carry

    lax.fori_loop(0, NH, wo_fin, 0)
    out_wo = pltpu.make_async_copy(pw.at[2], dwo_out, lsem.at[0])
    out_wo.start()
    kv_service(2)
    for i in range(2):
        r = pl.ds(i * (BLK // 2), BLK // 2)
        py_copy(i).wait_recv()
        dxo[r, :] = (pxo[r, :] + ry[r, :].astype(F32)).astype(BF16)
    out_dx = pltpu.make_async_copy(dxo, dx_out.at[0], lsem.at[1])
    out_dx.start()

    def wq_fin(h, carry):
        ring_final(S_WQ, 1, pq, h)
        return carry

    lax.fori_loop(0, NH, wq_fin, 0)
    out_wq = pltpu.make_async_copy(pq.at[2], dwq_out, lsem.at[2])
    out_wq.start()
    kv_copy(2).wait_recv()
    pkv[:, pl.ds(0, KC)] = pkv[:, kcol(3)] + rkv[2].astype(F32)
    out_kv = pltpu.make_async_copy(pkv.at[:, pl.ds(0, KC)], dwkv_out, lsem.at[3])
    out_kv.start()

    for i in range(NX):
        x_far(i, m).wait_send()
        x_fwd(i, far_m).wait_send()
    x_core(m).wait_send()
    for i in range(4):
        dy_far(i, m).wait_send()
        dy_fwd(i, far_m).wait_send()
    dy_core(m).wait_send()
    for base, which in ((S_WO, 0), (S_WQ, 1)):
        for hop in range(3):
            for h in range(NH):
                ring_copy(base, which, hop, h).wait_send()
    for hop in range(3):
        kv_copy(hop).wait_send()
    kp_copy.wait_send()
    for i in range(2):
        px_copy(i).wait_send()
        py_copy(i).wait_send()
    for cp in (out_wo, out_dx, out_wq, out_kv):
        cp.wait()


def solution(mesh):
    tok_spec = P(('pod', 'data'), 'model', None)

    def device_step(x_loc, dy_loc, w_q, w_k, w_v, w_o):
        any_spec = pl.BlockSpec(memory_space=pl.ANY)
        dx, dwq_t, dwkv_t, dwo = pl.pallas_call(
            step_kernel,
            out_shape=(jax.ShapeDtypeStruct((1, BLK, DIM), BF16), jax.ShapeDtypeStruct((HE, CH), F32),
                       jax.ShapeDtypeStruct((2 * HD, KC), F32), jax.ShapeDtypeStruct((HE, CH), F32)),
            in_specs=[any_spec] * 6,
            out_specs=[any_spec] * 4,
            scratch_shapes=[
                pltpu.VMEM((SEQ, DIM), BF16),
                pltpu.VMEM((SEQ, DIM), BF16),
                pltpu.VMEM((DIM, QKV), BF16),
                pltpu.VMEM((HE, DIM), BF16),
                pltpu.VMEM((SEQ, QKV), BF16),
                pltpu.VMEM((HD, SEQ), BF16),
                pltpu.VMEM((HD, SEQ), BF16),
                pltpu.VMEM((NH, CAUSAL_ROWS, BLK), F32),
                pltpu.VMEM((SEQ, BLK), BF16),
                pltpu.VMEM((HE, SEQ), BF16),
                pltpu.VMEM((SEQ, HE), BF16),
                pltpu.VMEM((QKV, SEQ), BF16),
                pltpu.VMEM((SEQ, QKV), BF16),
                pltpu.VMEM((SEQ, 2 * HD), F32),
                pltpu.VMEM((3, HE, CH), F32),
                pltpu.VMEM((3, HE, CH), F32),
                pltpu.VMEM((2 * HD, DIM // 2), F32),
                pltpu.VMEM((2 * HD, DIM // 2), BF16),
                pltpu.VMEM((2 * HD, DIM // 2), BF16),
                pltpu.VMEM((2, 3, NH, HD, CH), BF16),
                pltpu.VMEM((2, 3, NH, HD, CH), BF16),
                pltpu.VMEM((3, 2 * HD, KC), BF16),
                pltpu.VMEM((3, 2 * HD, KC), BF16),
                pltpu.VMEM((2, BLK, DIM), BF16),
                pltpu.VMEM((2, BLK, DIM), BF16),
                pltpu.VMEM((BLK, DIM), BF16),
                pltpu.VMEM((BLK, DIM), BF16),
                pltpu.VMEM((BLK, DIM), F32),
                pltpu.VMEM((BLK, DIM), F32),
                pltpu.VMEM((BLK, DIM), BF16),
                pltpu.SemaphoreType.DMA((N_SEM,)),
                pltpu.SemaphoreType.DMA((N_SEM,)),
                pltpu.SemaphoreType.DMA((6,)),
            ],
            compiler_params=pltpu.CompilerParams(collective_id=0, has_side_effects=True, vmem_limit_bytes=67043328),
        )(x_loc, dy_loc, w_q.reshape(DIM, HE), w_k, w_v, w_o.reshape(HE, DIM))
        dwq = dwq_t.T.reshape(CH, NH, HD)
        dwk = dwkv_t[:HD].T
        dwv = dwkv_t[HD:].T
        return dx, dwq, dwk, dwv, dwo.reshape(NH, HD, CH)

    kv_rows = P(('pod', 'model', 'data'), None)
    return jax.shard_map(device_step, mesh=mesh,
                         in_specs=(tok_spec, tok_spec, P(None, 'model', None), P(), P(), P('model', None, None)),
                         out_specs=(tok_spec, P(('pod', 'data'), 'model', None), kv_rows, kv_rows, P(('pod', 'model'), None, 'data')),
                         check_vma=False)
```

time: 412 us -> 129 us (0.31)
  waiting for transfers between devices: 288 us -> 0 us
  Pallas kernels: 0 us -> 119 us
  matrix products: 73.6 us -> 0 us
  between operations: 14.4 us -> 0.66 us
  local copies, waits for them, and re-layouts: 22.5 us -> 9.39 us
  other arithmetic: 12.3 us -> 0 us
    reduce_scatter x4 -> x0, waiting for transfers between devices: 225 us -> none  [the longest x1 76.7 us: device_step(): lax.psum_scatter(dwo_part, 'data', scatter_dimension=2, tiled=True)]
    pallas_call x0 -> x1, Pallas kernels: none -> 119 us  [device_step(): pl.pallas_call(step_kernel, out_shape=(jax.ShapeDtypeStruct((1, BLK, DIM)...]
    dot_general x13 -> x0, matrix products: 63 us -> none  [the longest x1 9.86 us: device_step(): jnp.einsum('bhqe,bke->bhqk', dout_loc, v_loc, preferred_element_type=jnp....]
    all_gather x2 -> x0, waiting for transfers between devices: 61.7 us -> none  [the longest x1 32.8 us: device_step(): dy_full = lax.all_gather(dy_loc, 'model', axis=1, tiled=True)]
    dynamic_slice x4 -> x0, local copies, waits for them, and re-layouts: 11.1 us -> none  [the longest x2 5.45 us: subgroup_scatter_sum(): lax.dynamic_index_in_dim(row_blocks, my_slot, axis=1, keepdims=False)]
    sub x1 -> x0, matrix products: 10.6 us -> none  [device_step(): attn_prob = jax.nn.softmax(jnp.where(causal, scores, -jnp.inf), axis=-1)]
    convert_element_type x2 -> x0, other arithmetic: 9.91 us -> none  [the longest x1 7.2 us: device_step(): prob_bf = attn_prob.astype(jnp.bfloat16)]
    unnamed x32 -> x12, local copies, waits for them, and re-layouts: 6.42 us -> 9.37 us
  transfers between devices with their start and end apart: 7 -> 0, of which waited for: 7 -> 0; matrix products, arithmetic and copies ran while one was open for 11% -> 0% of each run, Pallas kernels for 0% -> 0%
where the time goes in v1:
time: 129 us
  Pallas kernels  119 us (92%)
  local copies, waits for them, and re-layouts  9.39 us (7%)
    pallas_call x1, Pallas kernels, device_step(): pl.pallas_call(step_kernel, out_shape=(jax.ShapeDtypeStruct((1, BLK, DIM)...  119 us
    unnamed x12, local copies, waits for them, and re-layouts  9.37 us

profile of v1, /device:TPU:0, one launch (start us, length us, event | category | flops | bytes accessed | tf_op | source)
XLA Modules:
  0.0 129.2 jit_solution(12272000382184751443)
XLA Ops:
  0.6 3.3 %copy.16 = bf16[256,8,4,128]{3,1,2,0:T(8,128)(2,1)} copy(bf16[256,8,4,128]{3,2,1,0:T(4,128)(2,1)} %bitcast.14) | data formatting | bytes 4194304
  3.9 119.1 %shard_map.101 = (bf16[1,256,2048]{2,1,0:T(8,128)(2,1)}, f32[512,512]{1,0:T(8,128)}, f32[256,256]{1,0:T(8,128)}, f32[512,512]{1,0:T(8,128)}) custom-call(bf16[1,256,2048]{2,1,0:T(8,128)(2,1)} %x_in.1, bf16[1,256,2048]{2,1,0:T(8,128)(2,1)} %dy_in.1, bf16[2048,512]{1,0:T(8,128)(2,1)} %bitcast.13, bf16[2,2048,128]{2,1,0:T(8,128)(2,1)} %wk_in.1, ...), custom_call_target="tpu_custom_call" | custom-call | tf_op jit(solution)/shard_map/pallas_call | solution.py:398
  123.1 0.0 copy-start.2
  123.1 0.0 copy-start.1
  123.1 2.6 %copy.11 = f32[512,4,128]{2,1,0:T(4,128)} copy(f32[512,4,128]{0,2,1:T(8,128)} %bitcast.17) | data formatting | bytes 2097152
  125.7 0.0 copy-done.2
  125.7 0.0 copy-start
  125.7 0.8 copy.13
  126.5 0.8 copy.12
  127.3 0.0 copy-done.1
  127.3 1.0 copy.19
  128.2 0.0 copy-done
  128.2 1.0 copy.20
  (1 shorter events, 0.0 us)
Async XLA Ops:
  123.1 2.7 %copy-start.2 = (f32[256,256]{1,0:T(8,128)S(1)}, f32[256,256]{1,0:T(8,128)}, u32[]{:S(2)}) copy-start(f32[256,256]{1,0:T(8,128)} %get-tuple-element.11) | copy-start | bytes 786436
  123.1 4.2 %copy-start.1 = (bf16[1,256,2048]{2,1,0:T(8,128)(2,1)S(1)}, bf16[1,256,2048]{2,1,0:T(8,128)(2,1)}, u32[]{:S(2)}) copy-start(bf16[1,256,2048]{2,1,0:T(8,128)(2,1)} %get-tuple-element.25) | copy-start | bytes 3145732
  125.7 2.5 %copy-start = (f32[512,512]{1,0:T(8,128)S(1)}, f32[512,512]{1,0:T(8,128)}, u32[]{:S(2)}) copy-start(f32[512,512]{1,0:T(8,128)} %get-tuple-element.12) | copy-start | bytes 3145732

commit v2 on v1

--- a/solution.py
+++ b/solution.py
@@ -20,20 +20,22 @@
 HE = NH * HD
 QKV = HE + 2 * HD
 CH = 512
+SC = CH // 2
+WR = 1024
 KC = 256
-NX = 2
+NX = 4
 XR = BLK // NX
 NB = SEQ // BLK
 CAUSAL_ROWS = BLK * NB * (NB + 1) // 2
 
-S_XY, S_XF, S_XC = 0, 2, 4
-S_DY, S_DF, S_DC = 5, 9, 13
-S_WO, S_WQ = 14, 26
-S_KV = 38
-S_KP = 41
-S_PX = 42
-S_PY = 44
-N_SEM = 46
+S_XY, S_XF, S_XC = 0, 4, 8
+S_DY, S_DF, S_DC = 9, 14, 19
+S_WO, S_WQ = 20, 44
+S_KV = 68
+S_KP = 71
+S_PX = 72
+S_PY = 74
+N_SEM = 76
 
 
 def nn(a, b):
@@ -44,9 +46,9 @@
     return lax.dot_general(a, b, (((1,), (1,)), ((), ())), preferred_element_type=F32)
 
 
-def step_kernel(x_in, dy_in, wq_in, wk_in, wv_in, wo_in, dx_out, dwq_out, dwkv_out, dwo_out,
-                xg, dyg, wqkv, wo, qkv, kt, vt, prob, pbuf, ot, dout, at, am, dkv, pw, pq, pkv,
-                kvs, kvr, sring, rring, skv, rkv, sx, rx, sy, ry, pxo, pxm, dxo, ssem, rsem, lsem):
+def step_kernel(x_in, dy_in, wq_in, wk_in, wv_in, wo_in, dx_out, dwq_out, dwk_out, dwv_out, dwo_out,
+                xg, dyg, wq8, wst, wqkv, wo, qkv, kt, vt, prob, pbuf, ot, dout, at, am, dkv, pw, pq, pkv,
+                kvs, kvr, sring, rring, skv, rkv, sx, rx, sy, ry, pxo, dxo, wqo, kvo, ssem, rsem, lsem):
     pod = lax.axis_index("pod")
     z = lax.axis_index("data")
     m = lax.axis_index("model")
@@ -66,6 +68,11 @@
     def col(i):
         return pl.ds(pl.multiple_of(((z + 3 - i) % 4) * CH, CH), CH)
 
+    def dcol(i):
+        if i < 2:
+            return pl.ds(pl.multiple_of(((z + 3) % 4) * CH + i * SC, SC), SC)
+        return col(i - 1)
+
     def remote(src, dst, sem, dev):
         return pltpu.make_async_remote_copy(src_ref=src, dst_ref=dst, send_sem=ssem.at[sem], recv_sem=rsem.at[sem],
                                             device_id=dev, device_id_type=MESH)
@@ -78,7 +85,7 @@
         pltpu.make_async_copy(dy_in.at[0], dyg.at[rows(m)], lsem.at[1]),
         pltpu.make_async_copy(wk_in.at[y], wqkv.at[:, pl.ds(HE, HD)], lsem.at[2]),
         pltpu.make_async_copy(wv_in.at[y], wqkv.at[:, pl.ds(HE + HD, HD)], lsem.at[3]),
-        pltpu.make_async_copy(wq_in, wqkv.at[:, pl.ds(0, HE)], lsem.at[4]),
+        pltpu.make_async_copy(wq_in, wq8, lsem.at[4]),
         pltpu.make_async_copy(wo_in, wo, lsem.at[5]),
     ]
     for ld in loads:
@@ -101,10 +108,10 @@
         return remote(xg.at[rows(block)], xg.at[rows(block)], S_XC, core_dev)
 
     def dy_far(i, block):
-        return remote(dyg.at[rows(block), col(i)], dyg.at[rows(block), col(i)], S_DY + i, far_dev)
+        return remote(dyg.at[rows(block), dcol(i)], dyg.at[rows(block), dcol(i)], S_DY + i, far_dev)
 
     def dy_fwd(i, block):
-        return remote(dyg.at[rows(block), col(i)], dyg.at[rows(block), col(i)], S_DF + i, core_dev)
+        return remote(dyg.at[rows(block), dcol(i)], dyg.at[rows(block), dcol(i)], S_DF + i, core_dev)
 
     def dy_core(block):
         return remote(dyg.at[rows(block)], dyg.at[rows(block)], S_DC, core_dev)
@@ -114,18 +121,33 @@
         x_far(i, m).start()
     x_core(m).start()
     loads[1].wait()
-    for i in range(4):
+    for i in range(5):
         dy_far(i, m).start()
     dy_core(m).start()
     for ld in loads[2:]:
         ld.wait()
 
+    def wq_block(i, carry):
+        wst[...] = wq8[pl.ds(pl.multiple_of(i * WR, WR), WR), :].astype(F32)
+        for h in range(NH):
+            wqkv[pl.ds(pl.multiple_of(i * (WR // NH), WR // NH), WR // NH), pl.ds(h * HD, HD)] = wst[pl.ds(h, WR // NH, stride=NH), :].astype(BF16)
+        return carry
+
+    lax.fori_loop(0, DIM * NH // WR, wq_block, 0)
+
     def project(r):
         qkv[r, :] = nn(xg[r, :], wqkv[...]).astype(BF16)
+
+    def flip(block):
+        r = rows(block)
+        kt[:, r] = qkv[r, pl.ds(HE, HD)].T
+        vt[:, r] = qkv[r, pl.ds(HE + HD, HD)].T
 
     project(rows(m))
     x_core(core_m).wait_recv()
     project(rows(core_m))
+    flip(m)
+    flip(core_m)
 
     def x_piece(i, carry):
         x_far(i, far_m).wait_recv()
@@ -137,16 +159,23 @@
 
     lax.fori_loop(0, NX, x_piece, 0)
 
-    kt[...] = qkv[:, pl.ds(HE, HD)].T
-    vt[...] = qkv[:, pl.ds(HE + HD, HD)].T
+    flip(far_m)
+    flip(diag_m)
     dy_core(core_m).wait_recv()
 
     def take_dy(i):
         dy_far(i, far_m).wait_recv()
         dy_fwd(i, far_m).start()
 
-    def ring_copy(base, which, hop, h):
-        return remote(sring.at[which, hop, h], rring.at[which, hop, h], base + hop * 4 + h, right_dev)
+    def ring_copy(base, which, hop, s, h):
+        return remote(sring.at[which, hop, s, h], rring.at[which, hop, s, h], base + hop * 8 + s * 4 + h, right_dev)
+
+    def half_col(s):
+        return pl.ds(s * SC, SC)
+
+    def wo_first(s, h):
+        sring[0, 0, s, h] = nn(ot[head_rows(h), :], dyg[:, dcol(s)]).astype(BF16)
+        ring_copy(S_WO, 0, 0, s, h).start()
 
     scale = HD ** -0.5
     exp_scale = scale * math.log2(math.e)
@@ -186,21 +215,32 @@
             take_dy(0)
             dy_fwd(0, diag_m).wait_recv()
 
-        sring[0, 0, h] = nn(ot[hr, :], dyg[:, col(0)]).astype(BF16)
-        ring_copy(S_WO, 0, 0, h).start()
+        wo_first(0, h)
+
+        @pl.when(h == 1)
+        def _():
+            take_dy(1)
+            dy_fwd(1, diag_m).wait_recv()
+            wo_first(1, 0)
+
+        @pl.when(h >= 1)
+        def _():
+            wo_first(1, h)
+
         return carry
 
     lax.fori_loop(0, NH, fwd_head, 0)
 
     def ring_service(base, which, own, hop, h):
-        ring_copy(base, which, hop - 1, h).wait_recv()
-        total = own[hop - 1, head_rows(h), :] + rring[which, hop - 1, h].astype(F32)
-        sring[which, hop, h] = total.astype(BF16)
-        ring_copy(base, which, hop, h).start()
-
-    def ring_final(base, which, own, h):
-        ring_copy(base, which, 2, h).wait_recv()
-        own[2, head_rows(h), :] = own[2, head_rows(h), :] + rring[which, 2, h].astype(F32)
+        for s in range(2):
+            ring_copy(base, which, hop - 1, s, h).wait_recv()
+            total = own[hop - 1, head_rows(h), half_col(s)] + rring[which, hop - 1, s, h].astype(F32)
+            sring[which, hop, s, h] = total.astype(BF16)
+            ring_copy(base, which, hop, s, h).start()
+
+    def ring_final(base, which, own, h, s):
+        ring_copy(base, which, 2, s, h).wait_recv()
+        return own[2, head_rows(h), half_col(s)] + rring[which, 2, s, h].astype(F32)
 
     def wo_own(i):
         pw[i - 1] = nn(ot[...], dyg[:, col(i)])
@@ -209,8 +249,8 @@
         pq[i - 1] = nn(at[pl.ds(0, HE), :], xg[:, col(i)])
 
     for i in range(1, 4):
-        take_dy(i)
-        dy_fwd(i, diag_m).wait_recv()
+        take_dy(i + 1)
+        dy_fwd(i + 1, diag_m).wait_recv()
         wo_own(i)
         if i < 3:
             for h in range(2):
@@ -251,8 +291,10 @@
         def _():
             ring_service(S_WO, 0, pw, 2, h + 2)
 
-        sring[1, 0, h] = nn(at[hr, :], xg[:, col(0)]).astype(BF16)
-        ring_copy(S_WQ, 1, 0, h).start()
+        first = nn(at[hr, :], xg[:, col(0)]).astype(BF16)
+        for s in range(2):
+            sring[1, 0, s, h] = first[:, s * SC:(s + 1) * SC]
+            ring_copy(S_WQ, 1, 0, s, h).start()
         return carry
 
     lax.fori_loop(0, NH, bwd_head, 0)
@@ -289,66 +331,61 @@
             ref[:, cs] = v
         return put
 
-    dx_part(diag_m, put_sx(0))
-    px_copy(0).start()
-    dx_part(far_m, put_ref(pxm))
-    px_copy(0).wait_recv()
-    for i in range(2):
-        r = pl.ds(i * (BLK // 2), BLK // 2)
-        sy[r, :] = (pxm[r, :] + rx[0, r, :].astype(F32)).astype(BF16)
-        py_copy(i).start()
-
-    wq_own(1)
-    for h in range(2):
-        ring_service(S_WQ, 1, pq, 1, h)
-
-    atk = at[pl.ds(HE, 2 * HD), :]
     half = DIM // 2
-    kvs[...] = nn(atk, xg[:, pl.ds(pl.multiple_of((1 - c) * half, half), half)]).astype(BF16)
-    kp_copy = remote(kvs, kvr, S_KP, core_dev)
-    kp_copy.start()
-    for h in range(2, 4):
-        ring_service(S_WQ, 1, pq, 1, h)
-    pkv[...] = nn(atk, xg[:, pl.ds(pl.multiple_of(c * half, half), half)])
-    kp_copy.wait_recv()
-    pkv[...] += kvr[...].astype(F32)
+
+    def kv_half(which):
+        return nn(at[pl.ds(HE, 2 * HD), :], xg[:, pl.ds(pl.multiple_of(which * half, half), half)])
 
     def kcol(i):
         return pl.ds(pl.multiple_of(((z + 3 - i) % 4) * KC, KC), KC)
 
     def kv_copy(hop):
         return remote(skv.at[hop], rkv.at[hop], S_KV + hop, right_dev)
-
-    skv[0] = pkv[:, kcol(0)].astype(BF16)
-    kv_copy(0).start()
-
-    wq_own(2)
-    for h in range(2):
-        ring_service(S_WQ, 1, pq, 2, h)
-    dx_part(core_m, put_sx(1))
-    px_copy(1).start()
-    for h in range(2, 4):
-        ring_service(S_WQ, 1, pq, 2, h)
 
     def kv_service(hop):
         kv_copy(hop - 1).wait_recv()
         skv[hop] = (pkv[:, kcol(hop)] + rkv[hop - 1].astype(F32)).astype(BF16)
         kv_copy(hop).start()
 
+    kvs[...] = kv_half(1 - c).astype(BF16)
+    kp_copy = remote(kvs, kvr, S_KP, core_dev)
+    kp_copy.start()
+    dx_part(diag_m, put_sx(0))
+    px_copy(0).start()
+    pkv[...] = kv_half(c)
+    kp_copy.wait_recv()
+    pkv[...] += kvr[...].astype(F32)
+    skv[0] = pkv[:, kcol(0)].astype(BF16)
+    kv_copy(0).start()
+    dx_part(far_m, put_ref(pxo))
+    px_copy(0).wait_recv()
+    for i in range(2):
+        r = pl.ds(i * (BLK // 2), BLK // 2)
+        sy[r, :] = (pxo[r, :] + rx[0, r, :].astype(F32)).astype(BF16)
+        py_copy(i).start()
+
+    wq_own(1)
+    for h in range(NH):
+        ring_service(S_WQ, 1, pq, 1, h)
     kv_service(1)
+    dx_part(core_m, put_sx(1))
+    px_copy(1).start()
+    wq_own(2)
+    for h in range(2):
+        ring_service(S_WQ, 1, pq, 2, h)
+    kv_service(2)
+    for h in range(2, NH):
+        ring_service(S_WQ, 1, pq, 2, h)
     wq_own(3)
     dx_part(m, put_ref(pxo))
     px_copy(1).wait_recv()
     pxo[...] += rx[1].astype(F32)
 
-    def wo_fin(h, carry):
-        ring_final(S_WO, 0, pw, h)
-        return carry
-
-    lax.fori_loop(0, NH, wo_fin, 0)
+    for h in range(NH):
+        for s in range(2):
+            pw[2, head_rows(h), half_col(s)] = ring_final(S_WO, 0, pw, h, s)
     out_wo = pltpu.make_async_copy(pw.at[2], dwo_out, lsem.at[0])
     out_wo.start()
-    kv_service(2)
     for i in range(2):
         r = pl.ds(i * (BLK // 2), BLK // 2)
         py_copy(i).wait_recv()
@@ -356,37 +393,45 @@
     out_dx = pltpu.make_async_copy(dxo, dx_out.at[0], lsem.at[1])
     out_dx.start()
 
-    def wq_fin(h, carry):
-        ring_final(S_WQ, 1, pq, h)
-        return carry
-
-    lax.fori_loop(0, NH, wq_fin, 0)
-    out_wq = pltpu.make_async_copy(pq.at[2], dwq_out, lsem.at[2])
+    def wq_fin(h):
+        for s in range(2):
+            wqo[pl.ds(s * SC * NH + h, SC, stride=NH), :] = ring_final(S_WQ, 1, pq, h, s).T
+
+    for h in range(2):
+        wq_fin(h)
+    kv_copy(2).wait_recv()
+    kv_sum = pkv[:, kcol(3)] + rkv[2].astype(F32)
+    kvo[0] = kv_sum[:HD].T
+    kvo[1] = kv_sum[HD:].T
+    out_k = pltpu.make_async_copy(kvo.at[0], dwk_out, lsem.at[3])
+    out_k.start()
+    out_v = pltpu.make_async_copy(kvo.at[1], dwv_out, lsem.at[4])
+    out_v.start()
+    for h in range(2, NH):
+        wq_fin(h)
+    out_wq = pltpu.make_async_copy(wqo, dwq_out, lsem.at[2])
     out_wq.start()
-    kv_copy(2).wait_recv()
-    pkv[:, pl.ds(0, KC)] = pkv[:, kcol(3)] + rkv[2].astype(F32)
-    out_kv = pltpu.make_async_copy(pkv.at[:, pl.ds(0, KC)], dwkv_out, lsem.at[3])
-    out_kv.start()
 
     for i in range(NX):
         x_far(i, m).wait_send()
         x_fwd(i, far_m).wait_send()
     x_core(m).wait_send()
-    for i in range(4):
+    for i in range(5):
         dy_far(i, m).wait_send()
         dy_fwd(i, far_m).wait_send()
     dy_core(m).wait_send()
     for base, which in ((S_WO, 0), (S_WQ, 1)):
         for hop in range(3):
             for h in range(NH):
-                ring_copy(base, which, hop, h).wait_send()
+                for s in range(2):
+                    ring_copy(base, which, hop, s, h).wait_send()
     for hop in range(3):
         kv_copy(hop).wait_send()
     kp_copy.wait_send()
     for i in range(2):
         px_copy(i).wait_send()
         py_copy(i).wait_send()
-    for cp in (out_wo, out_dx, out_wq, out_kv):
+    for cp in (out_wo, out_dx, out_wq, out_k, out_v):
         cp.wait()
 
 
@@ -395,15 +440,18 @@
 
     def device_step(x_loc, dy_loc, w_q, w_k, w_v, w_o):
         any_spec = pl.BlockSpec(memory_space=pl.ANY)
-        dx, dwq_t, dwkv_t, dwo = pl.pallas_call(
+        dx, dwq, dwk, dwv, dwo = pl.pallas_call(
             step_kernel,
-            out_shape=(jax.ShapeDtypeStruct((1, BLK, DIM), BF16), jax.ShapeDtypeStruct((HE, CH), F32),
-                       jax.ShapeDtypeStruct((2 * HD, KC), F32), jax.ShapeDtypeStruct((HE, CH), F32)),
+            out_shape=(jax.ShapeDtypeStruct((1, BLK, DIM), BF16), jax.ShapeDtypeStruct((CH * NH, HD), F32),
+                       jax.ShapeDtypeStruct((KC, HD), F32), jax.ShapeDtypeStruct((KC, HD), F32),
+                       jax.ShapeDtypeStruct((HE, CH), F32)),
             in_specs=[any_spec] * 6,
-            out_specs=[any_spec] * 4,
+            out_specs=[any_spec] * 5,
             scratch_shapes=[
                 pltpu.VMEM((SEQ, DIM), BF16),
                 pltpu.VMEM((SEQ, DIM), BF16),
+                pltpu.VMEM((DIM * NH, HD), BF16),
+                pltpu.VMEM((WR, HD), F32),
                 pltpu.VMEM((DIM, QKV), BF16),
                 pltpu.VMEM((HE, DIM), BF16),
                 pltpu.VMEM((SEQ, QKV), BF16),
@@ -421,8 +469,8 @@
                 pltpu.VMEM((2 * HD, DIM // 2), F32),
                 pltpu.VMEM((2 * HD, DIM // 2), BF16),
                 pltpu.VMEM((2 * HD, DIM // 2), BF16),
-                pltpu.VMEM((2, 3, NH, HD, CH), BF16),
-                pltpu.VMEM((2, 3, NH, HD, CH), BF16),
+                pltpu.VMEM((2, 3, 2, NH, HD, SC), BF16),
+                pltpu.VMEM((2, 3, 2, NH, HD, SC), BF16),
                 pltpu.VMEM((3, 2 * HD, KC), BF16),
                 pltpu.VMEM((3, 2 * HD, KC), BF16),
                 pltpu.VMEM((2, BLK, DIM), BF16),
@@ -430,18 +478,16 @@
                 pltpu.VMEM((BLK, DIM), BF16),
                 pltpu.VMEM((BLK, DIM), BF16),
                 pltpu.VMEM((BLK, DIM), F32),
-                pltpu.VMEM((BLK, DIM), F32),
                 pltpu.VMEM((BLK, DIM), BF16),
+                pltpu.VMEM((CH * NH, HD), F32),
+                pltpu.VMEM((2, KC, HD), F32),
                 pltpu.SemaphoreType.DMA((N_SEM,)),
                 pltpu.SemaphoreType.DMA((N_SEM,)),
                 pltpu.SemaphoreType.DMA((6,)),
             ],
             compiler_params=pltpu.CompilerParams(collective_id=0, has_side_effects=True, vmem_limit_bytes=67043328),
-        )(x_loc, dy_loc, w_q.reshape(DIM, HE), w_k, w_v, w_o.reshape(HE, DIM))
-        dwq = dwq_t.T.reshape(CH, NH, HD)
-        dwk = dwkv_t[:HD].T
-        dwv = dwkv_t[HD:].T
-        return dx, dwq, dwk, dwv, dwo.reshape(NH, HD, CH)
+        )(x_loc, dy_loc, w_q.reshape(DIM * NH, HD), w_k, w_v, w_o.reshape(HE, DIM))
+        return dx, dwq.reshape(CH, NH, HD), dwk, dwv, dwo.reshape(NH, HD, CH)
 
     kv_rows = P(('pod', 'model', 'data'), None)
     return jax.shard_map(device_step, mesh=mesh,

time: 129 us -> 124 us (0.961)
  local copies, waits for them, and re-layouts: 9.39 us -> 5.72 us
    unnamed x12 -> x13, local copies, waits for them, and re-layouts: 9.37 us -> 5.72 us
    pallas_call x1, Pallas kernels: 119 us -> 118 us  [device_step(): pl.pallas_call(step_kernel, out_shape=(jax.ShapeDtypeStruct((1, BLK, DIM)...]
where the time goes in v2:
time: 124 us
  Pallas kernels  118 us (95%)
  local copies, waits for them, and re-layouts  5.72 us (5%)
    pallas_call x1, Pallas kernels, device_step(): pl.pallas_call(step_kernel, out_shape=(jax.ShapeDtypeStruct((1, BLK, DIM)...  118 us
    unnamed x13, local copies, waits for them, and re-layouts  5.72 us

profile of v2, /device:TPU:0, one launch (start us, length us, event | category | flops | bytes accessed | tf_op | source)
XLA Modules:
  0.0 124.2 jit_solution(8024506884514887309)
XLA Ops:
  0.6 117.8 %shard_map.101 = (bf16[1,256,2048]{2,1,0:T(8,128)(2,1)}, f32[2048,128]{1,0:T(8,128)}, f32[256,128]{1,0:T(8,128)}, f32[256,128]{1,0:T(8,128)}, f32[512,512]{1,0:T(8,128)}) custom-call(bf16[1,256,2048]{2,1,0:T(8,128)(2,1)} %x_in.1, bf16[1,256,2048]{2,1,0:T(8,128)(2,1)} %dy_in.1, bf16[8192,128]{1,0:T(8,128)(2,1)} %bitcast.4, bf16[2,2048,128]{2,1,0:T(8,128)(2,1)} %wk_in.1, ...), custom_call_target="tpu_custom_call" | custom-call | tf_op jit(solution)/shard_map/pallas_call | solution.py:443
  118.5 0.0 copy-start.1
  118.5 0.0 copy-start.3
  118.5 0.0 copy-start.2
  118.5 0.0 copy-start
  118.5 2.5 %copy.16 = bf16[1,256,2048]{2,1,0:T(8,128)(2,1)} copy(bf16[1,256,2048]{2,1,0:T(8,128)(2,1)} %get-tuple-element.20) | data formatting | bytes 2097152
  121.0 0.0 copy-done.1
  121.0 1.0 copy.17
  121.9 0.0 copy-done.3
  121.9 0.7 copy.18
  122.6 0.0 copy-done.2
  122.6 0.7 copy.19
  123.3 0.0 copy-done
  123.3 1.0 copy.20
Async XLA Ops:
  118.5 2.5 %copy-start.1 = (f32[2048,128]{1,0:T(8,128)S(1)}, f32[2048,128]{1,0:T(8,128)}, u32[]{:S(2)}) copy-start(f32[2048,128]{1,0:T(8,128)} %get-tuple-element.11) | copy-start | bytes 3145732
  118.5 3.5 %copy-start.3 = (f32[256,128]{1,0:T(8,128)S(1)}, f32[256,128]{1,0:T(8,128)}, u32[]{:S(2)}) copy-start(f32[256,128]{1,0:T(8,128)} %get-tuple-element.22) | copy-start | bytes 393220
  118.5 4.1 %copy-start.2 = (f32[256,128]{1,0:T(8,128)S(1)}, f32[256,128]{1,0:T(8,128)}, u32[]{:S(2)}) copy-start(f32[256,128]{1,0:T(8,128)} %get-tuple-element.23) | copy-start | bytes 393220
  118.5 4.8 %copy-start = (f32[512,512]{1,0:T(8,128)S(1)}, f32[512,512]{1,0:T(8,128)}, u32[]{:S(2)}) copy-start(f32[512,512]{1,0:T(8,128)} %get-tuple-element.14) | copy-start | bytes 3145732

commit v3 on v2

--- a/solution.py
+++ b/solution.py
@@ -36,6 +36,8 @@
 S_PX = 72
 S_PY = 74
 N_SEM = 76
+OWN = ((0, 1, 2), (3, 0, 1))
+VMEM_LIMIT = 63 * 2 ** 20 - 3328 * 1024
 
 
 def nn(a, b):
@@ -46,9 +48,9 @@
     return lax.dot_general(a, b, (((1,), (1,)), ((), ())), preferred_element_type=F32)
 
 
-def step_kernel(x_in, dy_in, wq_in, wk_in, wv_in, wo_in, dx_out, dwq_out, dwk_out, dwv_out, dwo_out,
-                xg, dyg, wq8, wst, wqkv, wo, qkv, kt, vt, prob, pbuf, ot, dout, at, am, dkv, pw, pq, pkv,
-                kvs, kvr, sring, rring, skv, rkv, sx, rx, sy, ry, pxo, dxo, wqo, kvo, ssem, rsem, lsem):
+def step_kernel(x_in, dy_in, wq_in, wk_in, wv_in, wo_in, dxo, wqo, dko, dvo, woo,
+                xg, dyg, wq8, wst, wqkv, wo, qkv, kt, vt, prob, pbuf, ot, dout, at, am, dkv, pw, pkv,
+                kvs, kvr, sring, rring, skv, rkv, sx, rx, sy, ry, pxo, ssem, rsem, lsem):
     pod = lax.axis_index("pod")
     z = lax.axis_index("data")
     m = lax.axis_index("model")
@@ -166,6 +168,8 @@
     def take_dy(i):
         dy_far(i, far_m).wait_recv()
         dy_fwd(i, far_m).start()
+
+    take_dy(0)
 
     def ring_copy(base, which, hop, s, h):
         return remote(sring.at[which, hop, s, h], rring.at[which, hop, s, h], base + hop * 8 + s * 4 + h, right_dev)
@@ -212,16 +216,19 @@
 
         @pl.when(h == 0)
         def _():
-            take_dy(0)
             dy_fwd(0, diag_m).wait_recv()
 
         wo_first(0, h)
+
+        @pl.when(h == 0)
+        def _():
+            take_dy(1)
 
         @pl.when(h == 1)
         def _():
-            take_dy(1)
             dy_fwd(1, diag_m).wait_recv()
             wo_first(1, 0)
+            take_dy(2)
 
         @pl.when(h >= 1)
         def _():
@@ -231,30 +238,31 @@
 
     lax.fori_loop(0, NH, fwd_head, 0)
 
-    def ring_service(base, which, own, hop, h):
+    def ring_service(base, which, hop, h):
         for s in range(2):
             ring_copy(base, which, hop - 1, s, h).wait_recv()
-            total = own[hop - 1, head_rows(h), half_col(s)] + rring[which, hop - 1, s, h].astype(F32)
+            total = pw[OWN[which][hop - 1], head_rows(h), half_col(s)] + rring[which, hop - 1, s, h].astype(F32)
             sring[which, hop, s, h] = total.astype(BF16)
             ring_copy(base, which, hop, s, h).start()
 
-    def ring_final(base, which, own, h, s):
+    def ring_final(base, which, h, s):
         ring_copy(base, which, 2, s, h).wait_recv()
-        return own[2, head_rows(h), half_col(s)] + rring[which, 2, s, h].astype(F32)
+        return pw[OWN[which][2], head_rows(h), half_col(s)] + rring[which, 2, s, h].astype(F32)
 
     def wo_own(i):
         pw[i - 1] = nn(ot[...], dyg[:, col(i)])
 
     def wq_own(i):
-        pq[i - 1] = nn(at[pl.ds(0, HE), :], xg[:, col(i)])
+        pw[OWN[1][i - 1]] = nn(at[pl.ds(0, HE), :], xg[:, col(i)])
 
     for i in range(1, 4):
-        take_dy(i + 1)
+        if i > 1:
+            take_dy(i + 1)
         dy_fwd(i + 1, diag_m).wait_recv()
         wo_own(i)
         if i < 3:
             for h in range(2):
-                ring_service(S_WO, 0, pw, 1, 2 * (i - 1) + h)
+                ring_service(S_WO, 0, 1, 2 * (i - 1) + h)
 
     def dout_block(b, carry):
         r = rows(b)
@@ -263,7 +271,7 @@
 
     lax.fori_loop(0, NB, dout_block, 0)
     for h in range(2):
-        ring_service(S_WO, 0, pw, 2, h)
+        ring_service(S_WO, 0, 2, h)
 
     dkv[...] = jnp.zeros_like(dkv)
 
@@ -289,7 +297,7 @@
 
         @pl.when(h < 2)
         def _():
-            ring_service(S_WO, 0, pw, 2, h + 2)
+            ring_service(S_WO, 0, 2, h + 2)
 
         first = nn(at[hr, :], xg[:, col(0)]).astype(BF16)
         for s in range(2):
@@ -366,16 +374,16 @@
 
     wq_own(1)
     for h in range(NH):
-        ring_service(S_WQ, 1, pq, 1, h)
+        ring_service(S_WQ, 1, 1, h)
     kv_service(1)
     dx_part(core_m, put_sx(1))
     px_copy(1).start()
     wq_own(2)
     for h in range(2):
-        ring_service(S_WQ, 1, pq, 2, h)
+        ring_service(S_WQ, 1, 2, h)
     kv_service(2)
     for h in range(2, NH):
-        ring_service(S_WQ, 1, pq, 2, h)
+        ring_service(S_WQ, 1, 2, h)
     wq_own(3)
     dx_part(m, put_ref(pxo))
     px_copy(1).wait_recv()
@@ -383,34 +391,24 @@
 
     for h in range(NH):
         for s in range(2):
-            pw[2, head_rows(h), half_col(s)] = ring_final(S_WO, 0, pw, h, s)
-    out_wo = pltpu.make_async_copy(pw.at[2], dwo_out, lsem.at[0])
-    out_wo.start()
+            woo[head_rows(h), half_col(s)] = ring_final(S_WO, 0, h, s)
     for i in range(2):
         r = pl.ds(i * (BLK // 2), BLK // 2)
         py_copy(i).wait_recv()
         dxo[r, :] = (pxo[r, :] + ry[r, :].astype(F32)).astype(BF16)
-    out_dx = pltpu.make_async_copy(dxo, dx_out.at[0], lsem.at[1])
-    out_dx.start()
 
     def wq_fin(h):
         for s in range(2):
-            wqo[pl.ds(s * SC * NH + h, SC, stride=NH), :] = ring_final(S_WQ, 1, pq, h, s).T
+            wqo[pl.ds(s * SC * NH + h, SC, stride=NH), :] = ring_final(S_WQ, 1, h, s).T
 
     for h in range(2):
         wq_fin(h)
     kv_copy(2).wait_recv()
     kv_sum = pkv[:, kcol(3)] + rkv[2].astype(F32)
-    kvo[0] = kv_sum[:HD].T
-    kvo[1] = kv_sum[HD:].T
-    out_k = pltpu.make_async_copy(kvo.at[0], dwk_out, lsem.at[3])
-    out_k.start()
-    out_v = pltpu.make_async_copy(kvo.at[1], dwv_out, lsem.at[4])
-    out_v.start()
+    dko[...] = kv_sum[:HD].T
+    dvo[...] = kv_sum[HD:].T
     for h in range(2, NH):
         wq_fin(h)
-    out_wq = pltpu.make_async_copy(wqo, dwq_out, lsem.at[2])
-    out_wq.start()
 
     for i in range(NX):
         x_far(i, m).wait_send()
@@ -431,8 +429,6 @@
     for i in range(2):
         px_copy(i).wait_send()
         py_copy(i).wait_send()
-    for cp in (out_wo, out_dx, out_wq, out_k, out_v):
-        cp.wait()
 
 
 def solution(mesh):
@@ -440,13 +436,13 @@
 
     def device_step(x_loc, dy_loc, w_q, w_k, w_v, w_o):
         any_spec = pl.BlockSpec(memory_space=pl.ANY)
+        vmem_spec = pl.BlockSpec(memory_space=pltpu.VMEM)
+        outs = (((BLK, DIM), BF16), ((CH * NH, HD), F32), ((KC, HD), F32), ((KC, HD), F32), ((HE, CH), F32))
         dx, dwq, dwk, dwv, dwo = pl.pallas_call(
             step_kernel,
-            out_shape=(jax.ShapeDtypeStruct((1, BLK, DIM), BF16), jax.ShapeDtypeStruct((CH * NH, HD), F32),
-                       jax.ShapeDtypeStruct((KC, HD), F32), jax.ShapeDtypeStruct((KC, HD), F32),
-                       jax.ShapeDtypeStruct((HE, CH), F32)),
+            out_shape=tuple(pltpu.VMEM(shape, dtype) for shape, dtype in outs),
             in_specs=[any_spec] * 6,
-            out_specs=[any_spec] * 5,
+            out_specs=[vmem_spec] * 5,
             scratch_shapes=[
                 pltpu.VMEM((SEQ, DIM), BF16),
                 pltpu.VMEM((SEQ, DIM), BF16),
@@ -464,8 +460,7 @@
                 pltpu.VMEM((QKV, SEQ), BF16),
                 pltpu.VMEM((SEQ, QKV), BF16),
                 pltpu.VMEM((SEQ, 2 * HD), F32),
-                pltpu.VMEM((3, HE, CH), F32),
-                pltpu.VMEM((3, HE, CH), F32),
+                pltpu.VMEM((4, HE, CH), F32),
                 pltpu.VMEM((2 * HD, DIM // 2), F32),
                 pltpu.VMEM((2 * HD, DIM // 2), BF16),
                 pltpu.VMEM((2 * HD, DIM // 2), BF16),
@@ -478,16 +473,13 @@
                 pltpu.VMEM((BLK, DIM), BF16),
                 pltpu.VMEM((BLK, DIM), BF16),
                 pltpu.VMEM((BLK, DIM), F32),
-                pltpu.VMEM((BLK, DIM), BF16),
-                pltpu.VMEM((CH * NH, HD), F32),
-                pltpu.VMEM((2, KC, HD), F32),
                 pltpu.SemaphoreType.DMA((N_SEM,)),
                 pltpu.SemaphoreType.DMA((N_SEM,)),
                 pltpu.SemaphoreType.DMA((6,)),
             ],
-            compiler_params=pltpu.CompilerParams(collective_id=0, has_side_effects=True, vmem_limit_bytes=67043328),
+            compiler_params=pltpu.CompilerParams(collective_id=0, has_side_effects=True, vmem_limit_bytes=VMEM_LIMIT),
         )(x_loc, dy_loc, w_q.reshape(DIM * NH, HD), w_k, w_v, w_o.reshape(HE, DIM))
-        return dx, dwq.reshape(CH, NH, HD), dwk, dwv, dwo.reshape(NH, HD, CH)
+        return dx.reshape(1, BLK, DIM), dwq.reshape(CH, NH, HD), dwk, dwv, dwo.reshape(NH, HD, CH)
 
     kv_rows = P(('pod', 'model', 'data'), None)
     return jax.shard_map(device_step, mesh=mesh,

time: 124 us -> 123 us (level)
  local copies, waits for them, and re-layouts: 5.72 us -> 4.22 us
    unnamed x13 -> x5, local copies, waits for them, and re-layouts: 5.72 us -> 4.22 us
where the time goes in v3:
time: 123 us
  Pallas kernels  118 us (96%)
  local copies, waits for them, and re-layouts  4.22 us (3%)
    pallas_call x1, Pallas kernels, device_step(): pl.pallas_call(step_kernel, out_shape=tuple((pltpu.VMEM(shape, dtype) for...  118 us
    unnamed x5, local copies, waits for them, and re-layouts  4.22 us

profile of v3, /device:TPU:0, one launch (start us, length us, event | category | flops | bytes accessed | tf_op | source)
XLA Modules:
  0.0 123.3 jit_solution(8799000270792714201)
XLA Ops:
  0.6 118.4 %shard_map.101 = (bf16[256,2048]{1,0:T(8,128)(2,1)S(1)}, f32[2048,128]{1,0:T(8,128)S(1)}, f32[256,128]{1,0:T(8,128)S(1)}, f32[256,128]{1,0:T(8,128)S(1)}, f32[512,512]{1,0:T(8,128)S(1)}) custom-call(bf16[1,256,2048]{2,1,0:T(8,128)(2,1)} %x_in.1, bf16[1,256,2048]{2,1,0:T(8,128)(2,1)} %dy_in.1, bf16[8192,128]{1,0:T(8,128)(2,1)} %bitcast.8, ...), custom_call_target="tpu_custom_call" | custom-call | tf_op jit(solution)/shard_map/pallas_call | solution.py:441
  119.1 1.0 copy.16
  120.1 1.0 copy.17
  121.0 0.7 copy.18
  121.7 0.7 copy.19
  122.3 1.0 copy.20

commit v4 on v3

--- a/solution.py
+++ b/solution.py
@@ -429,6 +429,16 @@
     for i in range(2):
         px_copy(i).wait_send()
         py_copy(i).wait_send()
+
+
+def store_kernel(*refs):
+    n = len(refs) // 2
+    sem = refs[-1]
+    copies = [pltpu.make_async_copy(refs[i], refs[n + i], sem.at[i]) for i in range(n)]
+    for cp in copies:
+        cp.start()
+    for cp in copies:
+        cp.wait()
 
 
 def solution(mesh):
@@ -479,6 +489,14 @@
             ],
             compiler_params=pltpu.CompilerParams(collective_id=0, has_side_effects=True, vmem_limit_bytes=VMEM_LIMIT),
         )(x_loc, dy_loc, w_q.reshape(DIM * NH, HD), w_k, w_v, w_o.reshape(HE, DIM))
+        dx, dwq, dwk, dwv, dwo = pl.pallas_call(
+            store_kernel,
+            out_shape=tuple(jax.ShapeDtypeStruct(shape, dtype) for shape, dtype in outs),
+            in_specs=[any_spec] * 5,
+            out_specs=[any_spec] * 5,
+            scratch_shapes=[pltpu.SemaphoreType.DMA((5,))],
+            compiler_params=pltpu.CompilerParams(vmem_limit_bytes=2 ** 20),
+        )(dx, dwq, dwk, dwv, dwo)
         return dx.reshape(1, BLK, DIM), dwq.reshape(CH, NH, HD), dwk, dwv, dwo.reshape(NH, HD, CH)
 
     kv_rows = P(('pod', 'model', 'data'), None)

time: 123 us -> 121 us (0.984)
  local copies, waits for them, and re-layouts: 4.22 us -> 0 us
  Pallas kernels: 118 us -> 120 us
    unnamed x5 -> x0, local copies, waits for them, and re-layouts: 4.22 us -> none
    pallas_call x0 -> x1, Pallas kernels: none -> 1.79 us  [device_step(): pl.pallas_call(store_kernel, out_shape=tuple((jax.ShapeDtypeStruct(shape,...]
where the time goes in v4:
time: 121 us
  Pallas kernels  120 us (99%)
    pallas_call x1, Pallas kernels, device_step(): pl.pallas_call(step_kernel, out_shape=tuple((pltpu.VMEM(shape, dtype) for...  118 us

profile of v4, /device:TPU:0, one launch (start us, length us, event | category | flops | bytes accessed | tf_op | source)
XLA Modules:
  0.0 121.0 jit_solution(13268970789954730618)
XLA Ops:
  0.6 118.4 %shard_map.101 = (bf16[256,2048]{1,0:T(8,128)(2,1)S(1)}, f32[2048,128]{1,0:T(8,128)S(1)}, f32[256,128]{1,0:T(8,128)S(1)}, f32[256,128]{1,0:T(8,128)S(1)}, f32[512,512]{1,0:T(8,128)S(1)}) custom-call(bf16[1,256,2048]{2,1,0:T(8,128)(2,1)} %x_in.1, bf16[1,256,2048]{2,1,0:T(8,128)(2,1)} %dy_in.1, bf16[8192,128]{1,0:T(8,128)(2,1)} %bitcast.5, ...), custom_call_target="tpu_custom_call" | custom-call | tf_op jit(solution)/shard_map/pallas_call | solution.py:451
  119.1 1.8 %shard_map.102 = (bf16[256,2048]{1,0:T(8,128)(2,1)}, f32[2048,128]{1,0:T(8,128)}, f32[256,128]{1,0:T(8,128)}, f32[256,128]{1,0:T(8,128)}, f32[512,512]{1,0:T(8,128)}) custom-call(bf16[256,2048]{1,0:T(8,128)(2,1)S(1)} %get-tuple-element.15.refs_0_, f32[2048,128]{1,0:T(8,128)S(1)} %get-tuple-element.16.refs_1_, f32[256,128]{1,0:T(8,128)S(1)} %get-tuple-element.17.refs_2_, ...), custom_call_target="tpu_custom_call" | custom-call | tf_op jit(solution)/shard_map/pallas_call | solution.py:492

commit v5 on v4

--- a/solution.py
+++ b/solution.py
@@ -35,7 +35,10 @@
 S_KP = 71
 S_PX = 72
 S_PY = 74
-N_SEM = 76
+S_XN, S_XNC, S_XNF, S_XNG = 76, 77, 78, 79
+S_A = 80
+N_SEM = 83
+AH = 3
 OWN = ((0, 1, 2), (3, 0, 1))
 VMEM_LIMIT = 63 * 2 ** 20 - 3328 * 1024
 
@@ -50,7 +53,7 @@
 
 def step_kernel(x_in, dy_in, wq_in, wk_in, wv_in, wo_in, dxo, wqo, dko, dvo, woo,
                 xg, dyg, wq8, wst, wqkv, wo, qkv, kt, vt, prob, pbuf, ot, dout, at, am, dkv, pw, pkv,
-                kvs, kvr, sring, rring, skv, rkv, sx, rx, sy, ry, pxo, ssem, rsem, lsem):
+                kvs, kvr, sring, rring, skv, rkv, sx, rx, sy, ry, xn, abuf, ssem, rsem, lsem):
     pod = lax.axis_index("pod")
     z = lax.axis_index("data")
     m = lax.axis_index("model")
@@ -64,6 +67,15 @@
     right_dev = (pod, (z + 1) % 4, m)
     left_dev = (pod, (z + 3) % 4, m)
 
+    inner = ((z + 1) // 2) % 2
+    edge_nb = (pod, 1 + z // 3, m)
+    q_e = 3 * (z // 2)
+    q_oe = 3 - q_e
+    q_o = 3 - z
+    edge_dev = (pod, q_e, m)
+    other_dev = (pod, q_o, m)
+    x_off = CH * (1 - z // 2)
+
     def rows(block, n=BLK, off=0):
         return pl.ds(pl.multiple_of(block * BLK + off, n), n)
 
@@ -87,11 +99,15 @@
         pltpu.make_async_copy(dy_in.at[0], dyg.at[rows(m)], lsem.at[1]),
         pltpu.make_async_copy(wk_in.at[y], wqkv.at[:, pl.ds(HE, HD)], lsem.at[2]),
         pltpu.make_async_copy(wv_in.at[y], wqkv.at[:, pl.ds(HE + HD, HD)], lsem.at[3]),
-        pltpu.make_async_copy(wq_in, wq8, lsem.at[4]),
-        pltpu.make_async_copy(wo_in, wo, lsem.at[5]),
+        pltpu.make_async_copy(wo_in, wo, lsem.at[4]),
     ]
+    def wq_load(i):
+        return pltpu.make_async_copy(wq_in.at[pl.ds(pl.multiple_of(i * WR, WR), WR)], wq8.at[i % 2], lsem.at[5 + i % 2])
+
     for ld in loads:
         ld.start()
+    wq_load(0).start()
+    wq_load(1).start()
 
     barrier = pltpu.get_barrier_semaphore()
     for dev in (far_dev, core_dev, right_dev, left_dev):
@@ -118,9 +134,20 @@
     def dy_core(block):
         return remote(dyg.at[rows(block)], dyg.at[rows(block)], S_DC, core_dev)
 
+    def xn_edge(block):
+        return remote(xg.at[rows(block), pl.ds(pl.multiple_of(x_off, CH), 3 * CH)], xn.at[rows(block)], S_XN, edge_nb)
+
+    def xn_send(block, sem, dev):
+        return remote(xn.at[rows(block)], xn.at[rows(block)], sem, dev)
+
     loads[0].wait()
     for i in range(NX):
         x_far(i, m).start()
+
+    @pl.when(inner == 0)
+    def _():
+        xn_edge(m).start()
+
     x_core(m).start()
     loads[1].wait()
     for i in range(5):
@@ -130,7 +157,13 @@
         ld.wait()
 
     def wq_block(i, carry):
-        wst[...] = wq8[pl.ds(pl.multiple_of(i * WR, WR), WR), :].astype(F32)
+        wq_load(i).wait()
+        wst[...] = wq8[i % 2].astype(F32)
+
+        @pl.when(i + 2 < DIM * NH // WR)
+        def _():
+            wq_load(i + 2).start()
+
         for h in range(NH):
             wqkv[pl.ds(pl.multiple_of(i * (WR // NH), WR // NH), WR // NH), pl.ds(h * HD, HD)] = wst[pl.ds(h, WR // NH, stride=NH), :].astype(BF16)
         return carry
@@ -169,8 +202,6 @@
         dy_far(i, far_m).wait_recv()
         dy_fwd(i, far_m).start()
 
-    take_dy(0)
-
     def ring_copy(base, which, hop, s, h):
         return remote(sring.at[which, hop, s, h], rring.at[which, hop, s, h], base + hop * 8 + s * 4 + h, right_dev)
 
@@ -180,6 +211,12 @@
     def wo_first(s, h):
         sring[0, 0, s, h] = nn(ot[head_rows(h), :], dyg[:, dcol(s)]).astype(BF16)
         ring_copy(S_WO, 0, 0, s, h).start()
+
+    @pl.when(inner == 1)
+    def _():
+        xn_edge(m).wait_recv()
+        xn_send(m, S_XNF, far_dev).start()
+        xn_send(m, S_XNC, core_dev).start()
 
     scale = HD ** -0.5
     exp_scale = scale * math.log2(math.e)
@@ -213,22 +250,22 @@
                 pbuf[pl.ds(kj * BLK, BLK), :] = p.astype(BF16)
             n = (qi + 1) * BLK
             ot[hr, pl.ds(qi * BLK, BLK)] = nn(vt[:, pl.ds(0, n)], pbuf[pl.ds(0, n), :]).astype(BF16)
+            for at_h, at_q, piece in ((0, 2, 0), (1, 1, 1), (3, 0, 2)):
+                if qi == at_q:
+                    @pl.when(h == at_h)
+                    def _(piece=piece):
+                        take_dy(piece)
 
         @pl.when(h == 0)
         def _():
             dy_fwd(0, diag_m).wait_recv()
 
         wo_first(0, h)
-
-        @pl.when(h == 0)
-        def _():
-            take_dy(1)
 
         @pl.when(h == 1)
         def _():
             dy_fwd(1, diag_m).wait_recv()
             wo_first(1, 0)
-            take_dy(2)
 
         @pl.when(h >= 1)
         def _():
@@ -252,8 +289,52 @@
     def wo_own(i):
         pw[i - 1] = nn(ot[...], dyg[:, col(i)])
 
-    def wq_own(i):
-        pw[OWN[1][i - 1]] = nn(at[pl.ds(0, HE), :], xg[:, col(i)])
+    ring_rows = pl.ds(AH * HD, (NH - AH) * HD)
+
+    def wq_own(i, r):
+        pw[OWN[1][i - 1], r, :] = nn(at[r, :], xg[:, col(i)])
+
+    def a_copy(h):
+        r = head_rows(h)
+        return remote(at.at[r], abuf.at[r], S_A + h, edge_nb)
+
+    def swap_copy(k, s, h):
+        return remote(sring.at[1, k, s, h], rring.at[1, k, s, h], S_WQ + k * 8 + s * 4 + h, other_dev)
+
+    def outer_copy(s, h):
+        return remote(sring.at[1, 2, s, h], rring.at[1, 2, s, h], S_WQ + 16 + s * 4 + h, edge_dev)
+
+    def xcol(q):
+        return pl.ds(pl.multiple_of(q * CH, CH), CH)
+
+    def ncol(q):
+        return pl.ds(pl.multiple_of(q * CH - x_off, CH), CH)
+
+    def spot(k, s, h, n):
+        return 1 + k // 2, pl.ds(((k % 2) * 2 + s) * AH * HD + h * HD, n * HD)
+
+    def roles():
+        for k, q in enumerate((q_oe, q_o, q_e)):
+            v = nn(at[pl.ds(0, AH * HD), :], xg[:, xcol(q)])
+            for s in range(2):
+                j, r = spot(k, s, 0, AH)
+                prob[j, r, :] = v[:, s * SC:(s + 1) * SC]
+
+    def combine(h):
+        a_copy(h).wait_recv()
+        for k, q in enumerate((q_oe, q_o)):
+            v = nn(abuf[head_rows(h), :], xn[:, ncol(q)])
+            for s in range(2):
+                j, r = spot(k, s, h, 1)
+                sring[1, k, s, h] = (prob[j, r, :] + v[:, s * SC:(s + 1) * SC]).astype(BF16)
+                swap_copy(k, s, h).start()
+
+    def outer(h):
+        for s in range(2):
+            swap_copy(0, s, h).wait_recv()
+            j, r = spot(2, s, h, 1)
+            sring[1, 2, s, h] = (prob[j, r, :] + rring[1, 0, s, h].astype(F32)).astype(BF16)
+            outer_copy(s, h).start()
 
     for i in range(1, 4):
         if i > 1:
@@ -295,17 +376,29 @@
             at[hr, qr] = dq
             am[qr, hr] = dq.T
 
-        @pl.when(h < 2)
+        @pl.when((h < 2) & (inner == 1))
         def _():
             ring_service(S_WO, 0, 2, h + 2)
 
-        first = nn(at[hr, :], xg[:, col(0)]).astype(BF16)
-        for s in range(2):
-            sring[1, 0, s, h] = first[:, s * SC:(s + 1) * SC]
-            ring_copy(S_WQ, 1, 0, s, h).start()
+        @pl.when((h < AH) & (inner == 0))
+        def _():
+            a_copy(h).start()
+
+        @pl.when(h >= AH)
+        def _():
+            first = nn(at[hr, :], xg[:, col(0)]).astype(BF16)
+            for s in range(2):
+                sring[1, 0, s, h] = first[:, s * SC:(s + 1) * SC]
+                ring_copy(S_WQ, 1, 0, s, h).start()
+
         return carry
 
     lax.fori_loop(0, NH, bwd_head, 0)
+
+    @pl.when(inner == 0)
+    def _():
+        for h in range(2, NH):
+            ring_service(S_WO, 0, 2, h)
 
     dkb = (dkv[:, pl.ds(0, HD)] * scale).astype(BF16)
     dvb = dkv[:, pl.ds(HD, HD)].astype(BF16)
@@ -317,7 +410,7 @@
     def dx_part(block, put):
         def piece(i, carry):
             cs = pl.ds(pl.multiple_of(i * CH, CH), CH)
-            put(cs, nt(am[rows(block), :], wqkv[cs, :]))
+            put(i, cs, nt(am[rows(block), :], wqkv[cs, :]))
             return carry
 
         lax.fori_loop(0, DIM // CH, piece, 0)
@@ -329,15 +422,17 @@
         r = pl.ds(i * (BLK // 2), BLK // 2)
         return remote(sy.at[r], ry.at[r], S_PY + i, far_dev)
 
-    def put_sx(i):
-        def put(cs, v):
-            sx[i, :, cs] = v.astype(BF16)
+    def put_sx(j):
+        def put(i, cs, v):
+            sx[j, :, cs] = v.astype(BF16)
         return put
 
-    def put_ref(ref):
-        def put(cs, v):
-            ref[:, cs] = v
-        return put
+    def pxo(i, s):
+        return prob.at[0, pl.ds(pl.multiple_of((2 * i + s) * BLK, BLK), BLK)]
+
+    def put_own(i, cs, v):
+        for s in range(2):
+            pxo(i, s)[...] = v[:, s * SC:(s + 1) * SC]
 
     half = DIM // 2
 
@@ -365,50 +460,93 @@
     pkv[...] += kvr[...].astype(F32)
     skv[0] = pkv[:, kcol(0)].astype(BF16)
     kv_copy(0).start()
-    dx_part(far_m, put_ref(pxo))
+
+    @pl.when(inner == 1)
+    def _():
+        xn_send(far_m, S_XNF, far_dev).wait_recv()
+        xn_send(far_m, S_XNG, core_dev).start()
+        roles()
+
+    dx_part(far_m, put_own)
     px_copy(0).wait_recv()
     for i in range(2):
         r = pl.ds(i * (BLK // 2), BLK // 2)
-        sy[r, :] = (pxo[r, :] + rx[0, r, :].astype(F32)).astype(BF16)
+        for j in range(DIM // SC):
+            cs = pl.ds(j * SC, SC)
+            own = prob[0, pl.ds(j * BLK + i * (BLK // 2), BLK // 2), :]
+            sy[r, cs] = (own + rx[0, r, cs].astype(F32)).astype(BF16)
         py_copy(i).start()
 
-    wq_own(1)
-    for h in range(NH):
-        ring_service(S_WQ, 1, 1, h)
-    kv_service(1)
+    @pl.when(inner == 1)
+    def _():
+        xn_send(core_m, S_XNC, core_dev).wait_recv()
+        xn_send(diag_m, S_XNG, core_dev).wait_recv()
+        combine(0)
+        combine(1)
+        outer(0)
+        combine(2)
+        outer(1)
+
+    for i in (1, 2):
+        wq_own(i, ring_rows)
+    wq_own(3, pl.ds(0, HE))
     dx_part(core_m, put_sx(1))
     px_copy(1).start()
-    wq_own(2)
-    for h in range(2):
-        ring_service(S_WQ, 1, 2, h)
-    kv_service(2)
-    for h in range(2, NH):
-        ring_service(S_WQ, 1, 2, h)
-    wq_own(3)
-    dx_part(m, put_ref(pxo))
-    px_copy(1).wait_recv()
-    pxo[...] += rx[1].astype(F32)
-
+    dx_part(m, put_own)
     for h in range(NH):
         for s in range(2):
             woo[head_rows(h), half_col(s)] = ring_final(S_WO, 0, h, s)
+
+    for h in range(AH, NH):
+        ring_service(S_WQ, 1, 1, h)
+
+    @pl.when(inner == 1)
+    def _():
+        outer(2)
+
+    kv_service(1)
+
+    @pl.when(inner == 1)
+    def _():
+        pw[OWN[1][2], pl.ds(0, AH * HD), :] += nn(abuf[...], xn[:, ncol(z)])
+
+    for h in range(AH, NH):
+        ring_service(S_WQ, 1, 2, h)
+    kv_service(2)
+
+    px_copy(1).wait_recv()
     for i in range(2):
         r = pl.ds(i * (BLK // 2), BLK // 2)
         py_copy(i).wait_recv()
-        dxo[r, :] = (pxo[r, :] + ry[r, :].astype(F32)).astype(BF16)
-
-    def wq_fin(h):
+        for j in range(DIM // SC):
+            cs = pl.ds(j * SC, SC)
+            own = prob[0, pl.ds(j * BLK + i * (BLK // 2), BLK // 2), :]
+            dxo[r, cs] = (own + rx[1, r, cs].astype(F32) + ry[r, cs].astype(F32)).astype(BF16)
+
+    def wq_put(h, s, v):
+        wqo[pl.ds(s * SC * NH + h, SC, stride=NH), :] = v.T
+
+    @pl.when(inner == 1)
+    def _():
+        for h in range(AH):
+            for s in range(2):
+                swap_copy(1, s, h).wait_recv()
+                wq_put(h, s, pw[OWN[1][2], head_rows(h), half_col(s)] + rring[1, 1, s, h].astype(F32))
+
+    @pl.when(inner == 0)
+    def _():
+        for h in range(AH):
+            for s in range(2):
+                outer_copy(s, h).wait_recv()
+                wq_put(h, s, pw[OWN[1][2], head_rows(h), half_col(s)] + rring[1, 2, s, h].astype(F32))
+
+    for h in range(AH, NH):
         for s in range(2):
-            wqo[pl.ds(s * SC * NH + h, SC, stride=NH), :] = ring_final(S_WQ, 1, h, s).T
-
-    for h in range(2):
-        wq_fin(h)
+            wq_put(h, s, ring_final(S_WQ, 1, h, s))
     kv_copy(2).wait_recv()
     kv_sum = pkv[:, kcol(3)] + rkv[2].astype(F32)
     dko[...] = kv_sum[:HD].T
     dvo[...] = kv_sum[HD:].T
-    for h in range(2, NH):
-        wq_fin(h)
 
     for i in range(NX):
         x_far(i, m).wait_send()
@@ -418,11 +556,30 @@
         dy_far(i, m).wait_send()
         dy_fwd(i, far_m).wait_send()
     dy_core(m).wait_send()
-    for base, which in ((S_WO, 0), (S_WQ, 1)):
-        for hop in range(3):
+    for hop in range(3):
+        for s in range(2):
             for h in range(NH):
-                for s in range(2):
-                    ring_copy(base, which, hop, s, h).wait_send()
+                ring_copy(S_WO, 0, hop, s, h).wait_send()
+            for h in range(AH, NH):
+                ring_copy(S_WQ, 1, hop, s, h).wait_send()
+
+    @pl.when(inner == 0)
+    def _():
+        xn_edge(m).wait_send()
+        for h in range(AH):
+            a_copy(h).wait_send()
+
+    @pl.when(inner == 1)
+    def _():
+        xn_send(m, S_XNF, far_dev).wait_send()
+        xn_send(m, S_XNC, core_dev).wait_send()
+        xn_send(far_m, S_XNG, core_dev).wait_send()
+        for h in range(AH):
+            for s in range(2):
+                for k in range(2):
+                    swap_copy(k, s, h).wait_send()
+                outer_copy(s, h).wait_send()
+
     for hop in range(3):
         kv_copy(hop).wait_send()
     kp_copy.wait_send()
@@ -456,7 +613,7 @@
             scratch_shapes=[
                 pltpu.VMEM((SEQ, DIM), BF16),
                 pltpu.VMEM((SEQ, DIM), BF16),
-                pltpu.VMEM((DIM * NH, HD), BF16),
+                pltpu.VMEM((2, WR, HD), BF16),
                 pltpu.VMEM((WR, HD), F32),
                 pltpu.VMEM((DIM, QKV), BF16),
                 pltpu.VMEM((HE, DIM), BF16),
@@ -482,10 +639,11 @@
                 pltpu.VMEM((2, BLK, DIM), BF16),
                 pltpu.VMEM((BLK, DIM), BF16),
                 pltpu.VMEM((BLK, DIM), BF16),
-                pltpu.VMEM((BLK, DIM), F32),
+                pltpu.VMEM((SEQ, 3 * CH), BF16),
+                pltpu.VMEM((AH * HD, SEQ), BF16),
                 pltpu.SemaphoreType.DMA((N_SEM,)),
                 pltpu.SemaphoreType.DMA((N_SEM,)),
-                pltpu.SemaphoreType.DMA((6,)),
+                pltpu.SemaphoreType.DMA((7,)),
             ],
             compiler_params=pltpu.CompilerParams(collective_id=0, has_side_effects=True, vmem_limit_bytes=VMEM_LIMIT),
         )(x_loc, dy_loc, w_q.reshape(DIM * NH, HD), w_k, w_v, w_o.reshape(HE, DIM))

time: 121 us -> 124 us (1.025)
  the two profiles are of different devices: /device:TPU:0 before, /device:TPU:16 now
where the time goes in v5:
time: 124 us
  Pallas kernels  123 us (99%)
    pallas_call x1, Pallas kernels, device_step(): pl.pallas_call(step_kernel, out_shape=tuple((pltpu.VMEM(shape, dtype) for...  121 us

profile of v5, /device:TPU:16, one launch (start us, length us, event | category | flops | bytes accessed | tf_op | source)
XLA Modules:
  0.0 123.8 jit_solution(11149330163371771805)
XLA Ops:
  0.6 121.2 %shard_map.101 = (bf16[256,2048]{1,0:T(8,128)(2,1)S(1)}, f32[2048,128]{1,0:T(8,128)S(1)}, f32[256,128]{1,0:T(8,128)S(1)}, f32[256,128]{1,0:T(8,128)S(1)}, f32[512,512]{1,0:T(8,128)S(1)}) custom-call(bf16[1,256,2048]{2,1,0:T(8,128)(2,1)} %x_in.1, bf16[1,256,2048]{2,1,0:T(8,128)(2,1)} %dy_in.1, bf16[8192,128]{1,0:T(8,128)(2,1)} %bitcast.5, ...), custom_call_target="tpu_custom_call" | custom-call | tf_op jit(solution)/shard_map/pallas_call | solution.py:608
  121.9 1.8 %shard_map.102 = (bf16[256,2048]{1,0:T(8,128)(2,1)}, f32[2048,128]{1,0:T(8,128)}, f32[256,128]{1,0:T(8,128)}, f32[256,128]{1,0:T(8,128)}, f32[512,512]{1,0:T(8,128)}) custom-call(bf16[256,2048]{1,0:T(8,128)(2,1)S(1)} %get-tuple-element.15.refs_0_, f32[2048,128]{1,0:T(8,128)S(1)} %get-tuple-element.16.refs_1_, f32[256,128]{1,0:T(8,128)S(1)} %get-tuple-element.17.refs_2_, ...), custom_call_target="tpu_custom_call" | custom-call | tf_op jit(solution)/shard_map/pallas_call | solution.py:650

commit v6 on v5

--- a/solution.py
+++ b/solution.py
@@ -30,16 +30,15 @@
 
 S_XY, S_XF, S_XC = 0, 4, 8
 S_DY, S_DF, S_DC = 9, 14, 19
-S_WO, S_WQ = 20, 44
-S_KV = 68
-S_KP = 71
-S_PX = 72
-S_PY = 74
-S_XN, S_XNC, S_XNF, S_XNG = 76, 77, 78, 79
-S_A = 80
-N_SEM = 83
-AH = 3
-OWN = ((0, 1, 2), (3, 0, 1))
+S_KP = 20
+S_PX = 21
+S_PY = 23
+S_XN, S_XNC, S_XNF, S_XNG = 25, 26, 27, 28
+S_A = 29
+S_WO = 33
+S_WQ = 81
+S_KV = 105
+N_SEM = 111
 VMEM_LIMIT = 63 * 2 ** 20 - 3328 * 1024
 
 
@@ -53,7 +52,7 @@
 
 def step_kernel(x_in, dy_in, wq_in, wk_in, wv_in, wo_in, dxo, wqo, dko, dvo, woo,
                 xg, dyg, wq8, wst, wqkv, wo, qkv, kt, vt, prob, pbuf, ot, dout, at, am, dkv, pw, pkv,
-                kvs, kvr, sring, rring, skv, rkv, sx, rx, sy, ry, xn, abuf, ssem, rsem, lsem):
+                kvs, kvr, so, ro, sq, rq, skv, rkv, sx, rx, sy, ry, xn, abuf, ssem, rsem, lsem):
     pod = lax.axis_index("pod")
     z = lax.axis_index("data")
     m = lax.axis_index("model")
@@ -64,27 +63,24 @@
     diag_m = (core_m + 2) % 4
     core_dev = (pod, z, core_m)
     far_dev = (pod, z, far_m)
-    right_dev = (pod, (z + 1) % 4, m)
-    left_dev = (pod, (z + 3) % 4, m)
 
     inner = ((z + 1) // 2) % 2
-    edge_nb = (pod, 1 + z // 3, m)
-    q_e = 3 * (z // 2)
-    q_oe = 3 - q_e
-    q_o = 3 - z
-    edge_dev = (pod, q_e, m)
-    other_dev = (pod, q_o, m)
+    pair_dev = (pod, z + 1 - 2 * (z % 2), m)
+    other_dev = (pod, 3 - z, m)
     x_off = CH * (1 - z // 2)
 
     def rows(block, n=BLK, off=0):
         return pl.ds(pl.multiple_of(block * BLK + off, n), n)
 
+    def chunk(i):
+        return i + (1 - z // 2) * (3 - 2 * i)
+
     def col(i):
-        return pl.ds(pl.multiple_of(((z + 3 - i) % 4) * CH, CH), CH)
+        return pl.ds(pl.multiple_of(chunk(i) * CH, CH), CH)
 
     def dcol(i):
         if i < 2:
-            return pl.ds(pl.multiple_of(((z + 3) % 4) * CH + i * SC, SC), SC)
+            return pl.ds(pl.multiple_of(chunk(0) * CH + i * SC, SC), SC)
         return col(i - 1)
 
     def remote(src, dst, sem, dev):
@@ -110,9 +106,14 @@
     wq_load(1).start()
 
     barrier = pltpu.get_barrier_semaphore()
-    for dev in (far_dev, core_dev, right_dev, left_dev):
+    for dev in (far_dev, core_dev, pair_dev):
         pl.semaphore_signal(barrier, inc=1, device_id=dev, device_id_type=MESH)
-    pl.semaphore_wait(barrier, 4)
+
+    @pl.when(inner == 1)
+    def _():
+        pl.semaphore_signal(barrier, inc=1, device_id=other_dev, device_id_type=MESH)
+
+    pl.semaphore_wait(barrier, 3 + inner)
 
     def x_far(i, block):
         r = rows(block, XR, i * XR)
@@ -135,7 +136,7 @@
         return remote(dyg.at[rows(block)], dyg.at[rows(block)], S_DC, core_dev)
 
     def xn_edge(block):
-        return remote(xg.at[rows(block), pl.ds(pl.multiple_of(x_off, CH), 3 * CH)], xn.at[rows(block)], S_XN, edge_nb)
+        return remote(xg.at[rows(block), pl.ds(pl.multiple_of(x_off, CH), 3 * CH)], xn.at[rows(block)], S_XN, pair_dev)
 
     def xn_send(block, sem, dev):
         return remote(xn.at[rows(block)], xn.at[rows(block)], sem, dev)
@@ -202,15 +203,32 @@
         dy_far(i, far_m).wait_recv()
         dy_fwd(i, far_m).start()
 
-    def ring_copy(base, which, hop, s, h):
-        return remote(sring.at[which, hop, s, h], rring.at[which, hop, s, h], base + hop * 8 + s * 4 + h, right_dev)
+    def wo_sem(slot, s, h):
+        return S_WO + slot * 8 + s * 4 + h
+
+    def wo_edge(k, s, h):
+        return remote(so.at[k, s, h], ro.at[k, s, h], wo_sem(k, s, h), pair_dev)
+
+    def wo_swap(k, s, h):
+        return remote(so.at[k, s, h], ro.at[3 + k, s, h], wo_sem(3 + k, s, h), other_dev)
+
+    def wo_back(s, h):
+        return remote(so.at[2, s, h], ro.at[3, s, h], wo_sem(5, s, h), pair_dev)
 
     def half_col(s):
         return pl.ds(s * SC, SC)
 
     def wo_first(s, h):
-        sring[0, 0, s, h] = nn(ot[head_rows(h), :], dyg[:, dcol(s)]).astype(BF16)
-        ring_copy(S_WO, 0, 0, s, h).start()
+        v = nn(ot[head_rows(h), :], dyg[:, dcol(s)])
+
+        @pl.when(inner == 0)
+        def _():
+            so[0, s, h] = v.astype(BF16)
+            wo_edge(0, s, h).start()
+
+        @pl.when(inner == 1)
+        def _():
+            pw[0, head_rows(h), half_col(s)] = v
 
     @pl.when(inner == 1)
     def _():
@@ -275,75 +293,73 @@
 
     lax.fori_loop(0, NH, fwd_head, 0)
 
-    def ring_service(base, which, hop, h):
+    def wo_pass(k, h):
         for s in range(2):
-            ring_copy(base, which, hop - 1, s, h).wait_recv()
-            total = pw[OWN[which][hop - 1], head_rows(h), half_col(s)] + rring[which, hop - 1, s, h].astype(F32)
-            sring[which, hop, s, h] = total.astype(BF16)
-            ring_copy(base, which, hop, s, h).start()
-
-    def ring_final(base, which, h, s):
-        ring_copy(base, which, 2, s, h).wait_recv()
-        return pw[OWN[which][2], head_rows(h), half_col(s)] + rring[which, 2, s, h].astype(F32)
-
-    def wo_own(i):
-        pw[i - 1] = nn(ot[...], dyg[:, col(i)])
-
-    ring_rows = pl.ds(AH * HD, (NH - AH) * HD)
-
-    def wq_own(i, r):
-        pw[OWN[1][i - 1], r, :] = nn(at[r, :], xg[:, col(i)])
-
-    def a_copy(h):
-        r = head_rows(h)
-        return remote(at.at[r], abuf.at[r], S_A + h, edge_nb)
-
-    def swap_copy(k, s, h):
-        return remote(sring.at[1, k, s, h], rring.at[1, k, s, h], S_WQ + k * 8 + s * 4 + h, other_dev)
-
-    def outer_copy(s, h):
-        return remote(sring.at[1, 2, s, h], rring.at[1, 2, s, h], S_WQ + 16 + s * 4 + h, edge_dev)
-
-    def xcol(q):
-        return pl.ds(pl.multiple_of(q * CH, CH), CH)
-
-    def ncol(q):
-        return pl.ds(pl.multiple_of(q * CH - x_off, CH), CH)
-
-    def spot(k, s, h, n):
-        return 1 + k // 2, pl.ds(((k % 2) * 2 + s) * AH * HD + h * HD, n * HD)
-
-    def roles():
-        for k, q in enumerate((q_oe, q_o, q_e)):
-            v = nn(at[pl.ds(0, AH * HD), :], xg[:, xcol(q)])
+            wo_edge(k, s, h).wait_recv()
+            so[k, s, h] = (pw[k, head_rows(h), half_col(s)] + ro[k, s, h].astype(F32)).astype(BF16)
+            wo_swap(k, s, h).start()
+
+    def wo_return(h):
+        for s in range(2):
+            wo_swap(0, s, h).wait_recv()
+            so[2, s, h] = (pw[3, head_rows(h), half_col(s)] + ro[3, s, h].astype(F32)).astype(BF16)
+            wo_back(s, h).start()
+
+    def wo_send(k):
+        for h in range(NH):
             for s in range(2):
-                j, r = spot(k, s, 0, AH)
-                prob[j, r, :] = v[:, s * SC:(s + 1) * SC]
-
-    def combine(h):
-        a_copy(h).wait_recv()
-        for k, q in enumerate((q_oe, q_o)):
-            v = nn(abuf[head_rows(h), :], xn[:, ncol(q)])
-            for s in range(2):
-                j, r = spot(k, s, h, 1)
-                sring[1, k, s, h] = (prob[j, r, :] + v[:, s * SC:(s + 1) * SC]).astype(BF16)
-                swap_copy(k, s, h).start()
-
-    def outer(h):
-        for s in range(2):
-            swap_copy(0, s, h).wait_recv()
-            j, r = spot(2, s, h, 1)
-            sring[1, 2, s, h] = (prob[j, r, :] + rring[1, 0, s, h].astype(F32)).astype(BF16)
-            outer_copy(s, h).start()
+                so[k, s, h] = pw[k, head_rows(h), half_col(s)].astype(BF16)
+                wo_edge(k, s, h).start()
 
     for i in range(1, 4):
         if i > 1:
             take_dy(i + 1)
         dy_fwd(i + 1, diag_m).wait_recv()
-        wo_own(i)
+        pw[i] = nn(ot[...], dyg[:, col(i)])
         if i < 3:
-            for h in range(2):
-                ring_service(S_WO, 0, 1, 2 * (i - 1) + h)
+            @pl.when(inner == 0)
+            def _(i=i):
+                wo_send(i)
+
+            @pl.when(inner == 1)
+            def _(i=i):
+                for h in (2 * i - 2, 2 * i - 1):
+                    wo_pass(0, h)
+
+    def a_copy(h):
+        r = head_rows(h)
+        return remote(at.at[r], abuf.at[r], S_A + h, pair_dev)
+
+    def wq_swap(k, s, h):
+        return remote(sq.at[k, s, h], rq.at[k, s, h], S_WQ + k * 8 + s * 4 + h, other_dev)
+
+    def wq_back(s, h):
+        return remote(sq.at[2, s, h], rq.at[2, s, h], S_WQ + 16 + s * 4 + h, pair_dev)
+
+    def ncol(k):
+        return pl.ds(pl.multiple_of(chunk(k) * CH - x_off, CH), CH)
+
+    def spot(k, s, h=0, n=1):
+        return prob.at[1 + k // 2, pl.ds(((k % 2) * 2 + s) * HE + h * HD, n * HD)]
+
+    def wq_own(k, q):
+        v = nn(at[pl.ds(0, HE), :], xg[:, pl.ds(pl.multiple_of(q * CH, CH), CH)])
+        for s in range(2):
+            spot(k, s, 0, NH)[...] = v[:, s * SC:(s + 1) * SC]
+
+    def combine(h):
+        a_copy(h).wait_recv()
+        for k in range(2):
+            v = nn(abuf[head_rows(h), :], xn[:, ncol(k)])
+            for s in range(2):
+                sq[k, s, h] = (spot(k, s, h)[...] + v[:, s * SC:(s + 1) * SC]).astype(BF16)
+                wq_swap(k, s, h).start()
+
+    def outer(h):
+        for s in range(2):
+            wq_swap(0, s, h).wait_recv()
+            sq[2, s, h] = (spot(3, s, h)[...] + rq[0, s, h].astype(F32)).astype(BF16)
+            wq_back(s, h).start()
 
     def dout_block(b, carry):
         r = rows(b)
@@ -351,8 +367,6 @@
         return carry
 
     lax.fori_loop(0, NB, dout_block, 0)
-    for h in range(2):
-        ring_service(S_WO, 0, 2, h)
 
     dkv[...] = jnp.zeros_like(dkv)
 
@@ -376,29 +390,18 @@
             at[hr, qr] = dq
             am[qr, hr] = dq.T
 
-        @pl.when((h < 2) & (inner == 1))
-        def _():
-            ring_service(S_WO, 0, 2, h + 2)
-
-        @pl.when((h < AH) & (inner == 0))
+        @pl.when(inner == 0)
         def _():
             a_copy(h).start()
 
-        @pl.when(h >= AH)
-        def _():
-            first = nn(at[hr, :], xg[:, col(0)]).astype(BF16)
-            for s in range(2):
-                sring[1, 0, s, h] = first[:, s * SC:(s + 1) * SC]
-                ring_copy(S_WQ, 1, 0, s, h).start()
+        @pl.when(inner == 1)
+        def _():
+            wo_pass(1, h)
+            wo_return(h)
 
         return carry
 
     lax.fori_loop(0, NH, bwd_head, 0)
-
-    @pl.when(inner == 0)
-    def _():
-        for h in range(2, NH):
-            ring_service(S_WO, 0, 2, h)
 
     dkb = (dkv[:, pl.ds(0, HD)] * scale).astype(BF16)
     dvb = dkv[:, pl.ds(HD, HD)].astype(BF16)
@@ -439,16 +442,22 @@
     def kv_half(which):
         return nn(at[pl.ds(HE, 2 * HD), :], xg[:, pl.ds(pl.multiple_of(which * half, half), half)])
 
-    def kcol(i):
-        return pl.ds(pl.multiple_of(((z + 3 - i) % 4) * KC, KC), KC)
-
-    def kv_copy(hop):
-        return remote(skv.at[hop], rkv.at[hop], S_KV + hop, right_dev)
-
-    def kv_service(hop):
-        kv_copy(hop - 1).wait_recv()
-        skv[hop] = (pkv[:, kcol(hop)] + rkv[hop - 1].astype(F32)).astype(BF16)
-        kv_copy(hop).start()
+    def kcol(k):
+        return pl.ds(pl.multiple_of(chunk(k) * KC, KC), KC)
+
+    def kv_edge(k):
+        return remote(skv.at[k], rkv.at[k], S_KV + k, pair_dev)
+
+    def kv_swap(k):
+        return remote(skv.at[k], rkv.at[3 + k], S_KV + 3 + k, other_dev)
+
+    def kv_back():
+        return remote(skv.at[2], rkv.at[3], S_KV + 5, pair_dev)
+
+    def kv_pass(k):
+        kv_edge(k).wait_recv()
+        skv[k] = (pkv[:, kcol(k)] + rkv[k].astype(F32)).astype(BF16)
+        kv_swap(k).start()
 
     kvs[...] = kv_half(1 - c).astype(BF16)
     kp_copy = remote(kvs, kvr, S_KP, core_dev)
@@ -458,14 +467,18 @@
     pkv[...] = kv_half(c)
     kp_copy.wait_recv()
     pkv[...] += kvr[...].astype(F32)
-    skv[0] = pkv[:, kcol(0)].astype(BF16)
-    kv_copy(0).start()
-
+
+    @pl.when(inner == 0)
+    def _():
+        for k in range(3):
+            skv[k] = pkv[:, kcol(k)].astype(BF16)
+            kv_edge(k).start()
     @pl.when(inner == 1)
     def _():
         xn_send(far_m, S_XNF, far_dev).wait_recv()
         xn_send(far_m, S_XNG, core_dev).start()
-        roles()
+        wq_own(0, chunk(0))
+        wq_own(1, chunk(1))
 
     dx_part(far_m, put_own)
     px_copy(0).wait_recv()
@@ -482,37 +495,42 @@
         xn_send(core_m, S_XNC, core_dev).wait_recv()
         xn_send(diag_m, S_XNG, core_dev).wait_recv()
         combine(0)
+        wq_own(3, chunk(3))
         combine(1)
         outer(0)
-        combine(2)
-        outer(1)
-
-    for i in (1, 2):
-        wq_own(i, ring_rows)
-    wq_own(3, pl.ds(0, HE))
+
     dx_part(core_m, put_sx(1))
     px_copy(1).start()
     dx_part(m, put_own)
-    for h in range(NH):
+    wq_own(2, z)
+
+    @pl.when(inner == 1)
+    def _():
+        combine(2)
+        outer(1)
+        combine(3)
+        outer(2)
+        kv_pass(0)
+        v = nn(abuf[...], xn[:, ncol(2)])
         for s in range(2):
-            woo[head_rows(h), half_col(s)] = ring_final(S_WO, 0, h, s)
-
-    for h in range(AH, NH):
-        ring_service(S_WQ, 1, 1, h)
-
-    @pl.when(inner == 1)
-    def _():
-        outer(2)
-
-    kv_service(1)
-
-    @pl.when(inner == 1)
-    def _():
-        pw[OWN[1][2], pl.ds(0, AH * HD), :] += nn(abuf[...], xn[:, ncol(z)])
-
-    for h in range(AH, NH):
-        ring_service(S_WQ, 1, 2, h)
-    kv_service(2)
+            spot(2, s, 0, NH)[...] += v[:, s * SC:(s + 1) * SC]
+        outer(3)
+        kv_pass(1)
+        kv_swap(0).wait_recv()
+        skv[2] = (pkv[:, kcol(3)] + rkv[3].astype(F32)).astype(BF16)
+        kv_back().start()
+        for h in range(NH):
+            for s in range(2):
+                wo_edge(2, s, h).wait_recv()
+                wo_swap(1, s, h).wait_recv()
+                woo[head_rows(h), half_col(s)] = pw[2, head_rows(h), half_col(s)] + ro[2, s, h].astype(F32) + ro[4, s, h].astype(F32)
+
+    @pl.when(inner == 0)
+    def _():
+        for h in range(NH):
+            for s in range(2):
+                wo_back(s, h).wait_recv()
+                woo[head_rows(h), half_col(s)] = pw[3, head_rows(h), half_col(s)] + ro[3, s, h].astype(F32)
 
     px_copy(1).wait_recv()
     for i in range(2):
@@ -523,30 +541,31 @@
             own = prob[0, pl.ds(j * BLK + i * (BLK // 2), BLK // 2), :]
             dxo[r, cs] = (own + rx[1, r, cs].astype(F32) + ry[r, cs].astype(F32)).astype(BF16)
 
-    def wq_put(h, s, v):
-        wqo[pl.ds(s * SC * NH + h, SC, stride=NH), :] = v.T
+    def wq_put(h, s, got):
+        wqo[pl.ds(s * SC * NH + h, SC, stride=NH), :] = (spot(2, s, h)[...] + got.astype(F32)).T
+
+    def kv_put(v):
+        dko[...] = v[:HD].T
+        dvo[...] = v[HD:].T
 
     @pl.when(inner == 1)
     def _():
-        for h in range(AH):
+        for h in range(NH):
             for s in range(2):
-                swap_copy(1, s, h).wait_recv()
-                wq_put(h, s, pw[OWN[1][2], head_rows(h), half_col(s)] + rring[1, 1, s, h].astype(F32))
+                wq_swap(1, s, h).wait_recv()
+                wq_put(h, s, rq[1, s, h])
+        kv_edge(2).wait_recv()
+        kv_swap(1).wait_recv()
+        kv_put(pkv[:, kcol(2)] + rkv[2].astype(F32) + rkv[4].astype(F32))
 
     @pl.when(inner == 0)
     def _():
-        for h in range(AH):
+        for h in range(NH):
             for s in range(2):
-                outer_copy(s, h).wait_recv()
-                wq_put(h, s, pw[OWN[1][2], head_rows(h), half_col(s)] + rring[1, 2, s, h].astype(F32))
-
-    for h in range(AH, NH):
-        for s in range(2):
-            wq_put(h, s, ring_final(S_WQ, 1, h, s))
-    kv_copy(2).wait_recv()
-    kv_sum = pkv[:, kcol(3)] + rkv[2].astype(F32)
-    dko[...] = kv_sum[:HD].T
-    dvo[...] = kv_sum[HD:].T
+                wq_back(s, h).wait_recv()
+                wq_put(h, s, rq[2, s, h])
+        kv_back().wait_recv()
+        kv_put(pkv[:, kcol(3)] + rkv[3].astype(F32))
 
     for i in range(NX):
         x_far(i, m).wait_send()
@@ -556,32 +575,33 @@
         dy_far(i, m).wait_send()
         dy_fwd(i, far_m).wait_send()
     dy_core(m).wait_send()
-    for hop in range(3):
-        for s in range(2):
-            for h in range(NH):
-                ring_copy(S_WO, 0, hop, s, h).wait_send()
-            for h in range(AH, NH):
-                ring_copy(S_WQ, 1, hop, s, h).wait_send()
-
     @pl.when(inner == 0)
     def _():
         xn_edge(m).wait_send()
-        for h in range(AH):
+        for h in range(NH):
             a_copy(h).wait_send()
+        for k in range(3):
+            kv_edge(k).wait_send()
+            for s in range(2):
+                for h in range(NH):
+                    wo_edge(k, s, h).wait_send()
 
     @pl.when(inner == 1)
     def _():
         xn_send(m, S_XNF, far_dev).wait_send()
         xn_send(m, S_XNC, core_dev).wait_send()
         xn_send(far_m, S_XNG, core_dev).wait_send()
-        for h in range(AH):
-            for s in range(2):
+        for k in range(2):
+            kv_swap(k).wait_send()
+        kv_back().wait_send()
+        for s in range(2):
+            for h in range(NH):
                 for k in range(2):
-                    swap_copy(k, s, h).wait_send()
-                outer_copy(s, h).wait_send()
-
-    for hop in range(3):
-        kv_copy(hop).wait_send()
+                    wo_swap(k, s, h).wait_send()
+                    wq_swap(k, s, h).wait_send()
+                wo_back(s, h).wait_send()
+                wq_back(s, h).wait_send()
+
     kp_copy.wait_send()
     for i in range(2):
         px_copy(i).wait_send()
@@ -631,16 +651,18 @@
                 pltpu.VMEM((2 * HD, DIM // 2), F32),
                 pltpu.VMEM((2 * HD, DIM // 2), BF16),
                 pltpu.VMEM((2 * HD, DIM // 2), BF16),
-                pltpu.VMEM((2, 3, 2, NH, HD, SC), BF16),
-                pltpu.VMEM((2, 3, 2, NH, HD, SC), BF16),
+                pltpu.VMEM((3, 2, NH, HD, SC), BF16),
+                pltpu.VMEM((5, 2, NH, HD, SC), BF16),
+                pltpu.VMEM((3, 2, NH, HD, SC), BF16),
+                pltpu.VMEM((3, 2, NH, HD, SC), BF16),
                 pltpu.VMEM((3, 2 * HD, KC), BF16),
-                pltpu.VMEM((3, 2 * HD, KC), BF16),
+                pltpu.VMEM((5, 2 * HD, KC), BF16),
                 pltpu.VMEM((2, BLK, DIM), BF16),
                 pltpu.VMEM((2, BLK, DIM), BF16),
                 pltpu.VMEM((BLK, DIM), BF16),
                 pltpu.VMEM((BLK, DIM), BF16),
                 pltpu.VMEM((SEQ, 3 * CH), BF16),
-                pltpu.VMEM((AH * HD, SEQ), BF16),
+                pltpu.VMEM((HE, SEQ), BF16),
                 pltpu.SemaphoreType.DMA((N_SEM,)),
                 pltpu.SemaphoreType.DMA((N_SEM,)),
                 pltpu.SemaphoreType.DMA((7,)),

time: 124 us -> 116 us (0.935)
  the two profiles are of different devices: /device:TPU:16 before, /device:TPU:0 now
where the time goes in v6:
time: 116 us
  Pallas kernels  115 us (99%)
    pallas_call x1, Pallas kernels, device_step(): pl.pallas_call(step_kernel, out_shape=tuple((pltpu.VMEM(shape, dtype) for...  113 us

profile of v6, /device:TPU:0, one launch (start us, length us, event | category | flops | bytes accessed | tf_op | source)
XLA Modules:
  0.0 115.8 jit_solution(14897127624389111197)
XLA Ops:
  0.6 113.2 %shard_map.101 = (bf16[256,2048]{1,0:T(8,128)(2,1)S(1)}, f32[2048,128]{1,0:T(8,128)S(1)}, f32[256,128]{1,0:T(8,128)S(1)}, f32[256,128]{1,0:T(8,128)S(1)}, f32[512,512]{1,0:T(8,128)S(1)}) custom-call(bf16[1,256,2048]{2,1,0:T(8,128)(2,1)} %x_in.1, bf16[1,256,2048]{2,1,0:T(8,128)(2,1)} %dy_in.1, bf16[8192,128]{1,0:T(8,128)(2,1)} %bitcast.5, ...), custom_call_target="tpu_custom_call" | custom-call | tf_op jit(solution)/shard_map/pallas_call | solution.py:628
  113.8 1.8 %shard_map.102 = (bf16[256,2048]{1,0:T(8,128)(2,1)}, f32[2048,128]{1,0:T(8,128)}, f32[256,128]{1,0:T(8,128)}, f32[256,128]{1,0:T(8,128)}, f32[512,512]{1,0:T(8,128)}) custom-call(bf16[256,2048]{1,0:T(8,128)(2,1)S(1)} %get-tuple-element.15.refs_0_, f32[2048,128]{1,0:T(8,128)S(1)} %get-tuple-element.16.refs_1_, f32[256,128]{1,0:T(8,128)S(1)} %get-tuple-element.17.refs_2_, ...), custom_call_target="tpu_custom_call" | custom-call | tf_op jit(solution)/shard_map/pallas_call | solution.py:672

commit v7 on v6

--- a/solution.py
+++ b/solution.py
@@ -38,7 +38,7 @@
 S_WO = 33
 S_WQ = 81
 S_KV = 105
-N_SEM = 111
+N_SEM = 117
 VMEM_LIMIT = 63 * 2 ** 20 - 3328 * 1024
 
 
@@ -219,7 +219,7 @@
         return pl.ds(s * SC, SC)
 
     def wo_first(s, h):
-        v = nn(ot[head_rows(h), :], dyg[:, dcol(s)])
+        v = nn(ot[pl.ds(h * HD, HD), :], dyg[:, dcol(s)])
 
         @pl.when(inner == 0)
         def _():
@@ -243,9 +243,9 @@
     def prow(qi, kj):
         return pl.ds(BLK * (qi * (qi + 1) // 2 + kj), BLK)
 
-    def fwd_head(h, carry):
-        hr = head_rows(h)
-        for qi in range(NB):
+    def fwd_head(h, first_q, last_q):
+        hr = pl.ds(h * HD, HD)
+        for qi in range(first_q, last_q):
             qb = qkv[pl.ds(qi * BLK, BLK), hr]
             mx = None
             for kj in range(qi + 1):
@@ -268,30 +268,26 @@
                 pbuf[pl.ds(kj * BLK, BLK), :] = p.astype(BF16)
             n = (qi + 1) * BLK
             ot[hr, pl.ds(qi * BLK, BLK)] = nn(vt[:, pl.ds(0, n)], pbuf[pl.ds(0, n), :]).astype(BF16)
-            for at_h, at_q, piece in ((0, 2, 0), (1, 1, 1), (3, 0, 2)):
-                if qi == at_q:
-                    @pl.when(h == at_h)
-                    def _(piece=piece):
-                        take_dy(piece)
-
-        @pl.when(h == 0)
-        def _():
-            dy_fwd(0, diag_m).wait_recv()
-
-        wo_first(0, h)
-
-        @pl.when(h == 1)
-        def _():
-            dy_fwd(1, diag_m).wait_recv()
-            wo_first(1, 0)
-
-        @pl.when(h >= 1)
-        def _():
-            wo_first(1, h)
-
-        return carry
-
-    lax.fori_loop(0, NH, fwd_head, 0)
+
+    fwd_head(0, 0, 3)
+    take_dy(0)
+    fwd_head(0, 3, NB)
+    dy_fwd(0, diag_m).wait_recv()
+    wo_first(0, 0)
+    fwd_head(1, 0, 3)
+    take_dy(1)
+    fwd_head(1, 3, NB)
+    wo_first(0, 1)
+    dy_fwd(1, diag_m).wait_recv()
+    wo_first(1, 0)
+    wo_first(1, 1)
+    for h in range(2, NH):
+        fwd_head(h, 0, 3)
+        if h == 3:
+            take_dy(2)
+        fwd_head(h, 3, NB)
+        for s in range(2):
+            wo_first(s, h)
 
     def wo_pass(k, h):
         for s in range(2):
@@ -347,9 +343,10 @@
         for s in range(2):
             spot(k, s, 0, NH)[...] = v[:, s * SC:(s + 1) * SC]
 
-    def combine(h):
-        a_copy(h).wait_recv()
-        for k in range(2):
+    def combine(h, ks=(0, 1)):
+        if 0 in ks:
+            a_copy(h).wait_recv()
+        for k in ks:
             v = nn(abuf[head_rows(h), :], xn[:, ncol(k)])
             for s in range(2):
                 sq[k, s, h] = (spot(k, s, h)[...] + v[:, s * SC:(s + 1) * SC]).astype(BF16)
@@ -445,19 +442,26 @@
     def kcol(k):
         return pl.ds(pl.multiple_of(chunk(k) * KC, KC), KC)
 
-    def kv_edge(k):
-        return remote(skv.at[k], rkv.at[k], S_KV + k, pair_dev)
-
-    def kv_swap(k):
-        return remote(skv.at[k], rkv.at[3 + k], S_KV + 3 + k, other_dev)
-
-    def kv_back():
-        return remote(skv.at[2], rkv.at[3], S_KV + 5, pair_dev)
+    def kv_part(ref, slot, t):
+        return ref.at[slot, pl.ds(t * HD, HD)]
+
+    def kv_edge(k, t):
+        return remote(kv_part(skv, k, t), kv_part(rkv, k, t), S_KV + 2 * k + t, pair_dev)
+
+    def kv_swap(k, t):
+        return remote(kv_part(skv, k, t), kv_part(rkv, 3 + k, t), S_KV + 2 * (3 + k) + t, other_dev)
+
+    def kv_back(t):
+        return remote(kv_part(skv, 2, t), kv_part(rkv, 3, t), S_KV + 10 + t, pair_dev)
+
+    def kv_own(k, t):
+        return pkv[pl.ds(t * HD, HD), kcol(k)]
 
     def kv_pass(k):
-        kv_edge(k).wait_recv()
-        skv[k] = (pkv[:, kcol(k)] + rkv[k].astype(F32)).astype(BF16)
-        kv_swap(k).start()
+        for t in range(2):
+            kv_edge(k, t).wait_recv()
+            kv_part(skv, k, t)[...] = (kv_own(k, t) + kv_part(rkv, k, t)[...].astype(F32)).astype(BF16)
+            kv_swap(k, t).start()
 
     kvs[...] = kv_half(1 - c).astype(BF16)
     kp_copy = remote(kvs, kvr, S_KP, core_dev)
@@ -471,8 +475,9 @@
     @pl.when(inner == 0)
     def _():
         for k in range(3):
-            skv[k] = pkv[:, kcol(k)].astype(BF16)
-            kv_edge(k).start()
+            for t in range(2):
+                kv_part(skv, k, t)[...] = kv_own(k, t).astype(BF16)
+                kv_edge(k, t).start()
     @pl.when(inner == 1)
     def _():
         xn_send(far_m, S_XNF, far_dev).wait_recv()
@@ -508,17 +513,19 @@
     def _():
         combine(2)
         outer(1)
-        combine(3)
+        combine(3, (0,))
         outer(2)
+        v = nn(abuf[...], xn[:, ncol(2)])
+        for s in range(2):
+            spot(2, s, 0, NH)[...] += v[:, s * SC:(s + 1) * SC]
         kv_pass(0)
-        v = nn(abuf[...], xn[:, ncol(2)])
-        for s in range(2):
-            spot(2, s, 0, NH)[...] += v[:, s * SC:(s + 1) * SC]
+        combine(3, (1,))
         outer(3)
         kv_pass(1)
-        kv_swap(0).wait_recv()
-        skv[2] = (pkv[:, kcol(3)] + rkv[3].astype(F32)).astype(BF16)
-        kv_back().start()
+        for t in range(2):
+            kv_swap(0, t).wait_recv()
+            kv_part(skv, 2, t)[...] = (kv_own(3, t) + kv_part(rkv, 3, t)[...].astype(F32)).astype(BF16)
+            kv_back(t).start()
         for h in range(NH):
             for s in range(2):
                 wo_edge(2, s, h).wait_recv()
@@ -544,9 +551,7 @@
     def wq_put(h, s, got):
         wqo[pl.ds(s * SC * NH + h, SC, stride=NH), :] = (spot(2, s, h)[...] + got.astype(F32)).T
 
-    def kv_put(v):
-        dko[...] = v[:HD].T
-        dvo[...] = v[HD:].T
+    kv_out = (dko, dvo)
 
     @pl.when(inner == 1)
     def _():
@@ -554,9 +559,10 @@
             for s in range(2):
                 wq_swap(1, s, h).wait_recv()
                 wq_put(h, s, rq[1, s, h])
-        kv_edge(2).wait_recv()
-        kv_swap(1).wait_recv()
-        kv_put(pkv[:, kcol(2)] + rkv[2].astype(F32) + rkv[4].astype(F32))
+        for t in range(2):
+            kv_edge(2, t).wait_recv()
+            kv_swap(1, t).wait_recv()
+            kv_out[t][...] = (kv_own(2, t) + kv_part(rkv, 2, t)[...].astype(F32) + kv_part(rkv, 4, t)[...].astype(F32)).T
 
     @pl.when(inner == 0)
     def _():
@@ -564,8 +570,9 @@
             for s in range(2):
                 wq_back(s, h).wait_recv()
                 wq_put(h, s, rq[2, s, h])
-        kv_back().wait_recv()
-        kv_put(pkv[:, kcol(3)] + rkv[3].astype(F32))
+        for t in range(2):
+            kv_back(t).wait_recv()
+            kv_out[t][...] = (kv_own(3, t) + kv_part(rkv, 3, t)[...].astype(F32)).T
 
     for i in range(NX):
         x_far(i, m).wait_send()
@@ -581,7 +588,8 @@
         for h in range(NH):
             a_copy(h).wait_send()
         for k in range(3):
-            kv_edge(k).wait_send()
+            for t in range(2):
+                kv_edge(k, t).wait_send()
             for s in range(2):
                 for h in range(NH):
                     wo_edge(k, s, h).wait_send()
@@ -591,9 +599,10 @@
         xn_send(m, S_XNF, far_dev).wait_send()
         xn_send(m, S_XNC, core_dev).wait_send()
         xn_send(far_m, S_XNG, core_dev).wait_send()
-        for k in range(2):
-            kv_swap(k).wait_send()
-        kv_back().wait_send()
+        for t in range(2):
+            for k in range(2):
+                kv_swap(k, t).wait_send()
+            kv_back(t).wait_send()
         for s in range(2):
             for h in range(NH):
                 for k in range(2):

time: 116 us -> 112 us (0.966)
  Pallas kernels: 115 us -> 111 us
    pallas_call x1, Pallas kernels: 113 us -> 109 us  [device_step(): pl.pallas_call(step_kernel, out_shape=tuple((pltpu.VMEM(shape, dtype) for...]
where the time goes in v7:
time: 112 us
  Pallas kernels  111 us (99%)
    pallas_call x1, Pallas kernels, device_step(): pl.pallas_call(step_kernel, out_shape=tuple((pltpu.VMEM(shape, dtype) for...  109 us

profile of v7, /device:TPU:0, one launch (start us, length us, event | category | flops | bytes accessed | tf_op | source)
XLA Modules:
  0.0 111.7 jit_solution(15917401226187576254)
XLA Ops:
  0.6 109.1 %shard_map.101 = (bf16[256,2048]{1,0:T(8,128)(2,1)S(1)}, f32[2048,128]{1,0:T(8,128)S(1)}, f32[256,128]{1,0:T(8,128)S(1)}, f32[256,128]{1,0:T(8,128)S(1)}, f32[512,512]{1,0:T(8,128)S(1)}) custom-call(bf16[1,256,2048]{2,1,0:T(8,128)(2,1)} %x_in.1, bf16[1,256,2048]{2,1,0:T(8,128)(2,1)} %dy_in.1, bf16[8192,128]{1,0:T(8,128)(2,1)} %bitcast.5, ...), custom_call_target="tpu_custom_call" | custom-call | tf_op jit(solution)/shard_map/pallas_call | solution.py:637
  109.7 1.8 %shard_map.102 = (bf16[256,2048]{1,0:T(8,128)(2,1)}, f32[2048,128]{1,0:T(8,128)}, f32[256,128]{1,0:T(8,128)}, f32[256,128]{1,0:T(8,128)}, f32[512,512]{1,0:T(8,128)}) custom-call(bf16[256,2048]{1,0:T(8,128)(2,1)S(1)} %get-tuple-element.15.refs_0_, f32[2048,128]{1,0:T(8,128)S(1)} %get-tuple-element.16.refs_1_, f32[256,128]{1,0:T(8,128)S(1)} %get-tuple-element.17.refs_2_, ...), custom_call_target="tpu_custom_call" | custom-call | tf_op jit(solution)/shard_map/pallas_call | solution.py:681

commit v8 on v7

--- a/solution.py
+++ b/solution.py
@@ -38,7 +38,9 @@
 S_WO = 33
 S_WQ = 81
 S_KV = 105
-N_SEM = 117
+S_XT, S_XU = 117, 121
+N_SEM = 125
+XT = XR // 4
 VMEM_LIMIT = 63 * 2 ** 20 - 3328 * 1024
 
 
@@ -52,7 +54,7 @@
 
 def step_kernel(x_in, dy_in, wq_in, wk_in, wv_in, wo_in, dxo, wqo, dko, dvo, woo,
                 xg, dyg, wq8, wst, wqkv, wo, qkv, kt, vt, prob, pbuf, ot, dout, at, am, dkv, pw, pkv,
-                kvs, kvr, so, ro, sq, rq, skv, rkv, sx, rx, sy, ry, xn, abuf, ssem, rsem, lsem):
+                kvs, kvr, so, ro, sq, rq, skv, rkv, sx, rx, sy, ry, xn, xta, xtb, abuf, ssem, rsem, lsem):
     pod = lax.axis_index("pod")
     z = lax.axis_index("data")
     m = lax.axis_index("model")
@@ -141,18 +143,34 @@
     def xn_send(block, sem, dev):
         return remote(xn.at[rows(block)], xn.at[rows(block)], sem, dev)
 
+    def xt_edge(j):
+        return remote(xg.at[rows(m, XT, (NX - 1) * XR + j * XT)], xta.at[pl.ds(j * XT, XT)], S_XT + j, pair_dev)
+
+    def xt_far(j):
+        return remote(xta.at[pl.ds(j * XT, XT)], xtb.at[pl.ds(j * XT, XT)], S_XU + j, far_dev)
+
+    def xt_back():
+        return remote(xtb, xg.at[rows(far_m, XR, (NX - 1) * XR)], S_XY + NX - 1, pair_dev)
+
     loads[0].wait()
-    for i in range(NX):
-        x_far(i, m).start()
+    x_far(0, m).start()
 
     @pl.when(inner == 0)
     def _():
+        for j in range(4):
+            xt_edge(j).start()
         xn_edge(m).start()
+        for i in range(1, NX - 1):
+            x_far(i, m).start()
 
     x_core(m).start()
     loads[1].wait()
-    for i in range(5):
-        dy_far(i, m).start()
+
+    @pl.when(inner == 0)
+    def _():
+        for i in range(5):
+            dy_far(i, m).start()
+
     dy_core(m).start()
     for ld in loads[2:]:
         ld.wait()
@@ -170,6 +188,16 @@
         return carry
 
     lax.fori_loop(0, DIM * NH // WR, wq_block, 0)
+
+    @pl.when(inner == 1)
+    def _():
+        for j in range(4):
+            xt_edge(j).wait_recv()
+            xt_far(j).start()
+        for i in range(1, NX):
+            x_far(i, m).start()
+        for i in range(5):
+            dy_far(i, m).start()
 
     def project(r):
         qkv[r, :] = nn(xg[r, :], wqkv[...]).astype(BF16)
@@ -184,6 +212,12 @@
     project(rows(core_m))
     flip(m)
     flip(core_m)
+
+    @pl.when(inner == 1)
+    def _():
+        for j in range(4):
+            xt_far(j).wait_recv()
+        xt_back().start()
 
     def x_piece(i, carry):
         x_far(i, far_m).wait_recv()
@@ -274,12 +308,13 @@
     fwd_head(0, 3, NB)
     dy_fwd(0, diag_m).wait_recv()
     wo_first(0, 0)
-    fwd_head(1, 0, 3)
+    fwd_head(1, 0, 2)
     take_dy(1)
+    fwd_head(1, 2, 3)
+    dy_fwd(1, diag_m).wait_recv()
+    wo_first(1, 0)
     fwd_head(1, 3, NB)
     wo_first(0, 1)
-    dy_fwd(1, diag_m).wait_recv()
-    wo_first(1, 0)
     wo_first(1, 1)
     for h in range(2, NH):
         fwd_head(h, 0, 3)
@@ -574,8 +609,9 @@
             kv_back(t).wait_recv()
             kv_out[t][...] = (kv_own(3, t) + kv_part(rkv, 3, t)[...].astype(F32)).T
 
+    for i in range(NX - 1):
+        x_far(i, m).wait_send()
     for i in range(NX):
-        x_far(i, m).wait_send()
         x_fwd(i, far_m).wait_send()
     x_core(m).wait_send()
     for i in range(5):
@@ -584,6 +620,8 @@
     dy_core(m).wait_send()
     @pl.when(inner == 0)
     def _():
+        for j in range(4):
+            xt_edge(j).wait_send()
         xn_edge(m).wait_send()
         for h in range(NH):
             a_copy(h).wait_send()
@@ -596,6 +634,10 @@
 
     @pl.when(inner == 1)
     def _():
+        x_far(NX - 1, m).wait_send()
+        for j in range(4):
+            xt_far(j).wait_send()
+        xt_back().wait_send()
         xn_send(m, S_XNF, far_dev).wait_send()
         xn_send(m, S_XNC, core_dev).wait_send()
         xn_send(far_m, S_XNG, core_dev).wait_send()
@@ -671,6 +713,8 @@
                 pltpu.VMEM((BLK, DIM), BF16),
                 pltpu.VMEM((BLK, DIM), BF16),
                 pltpu.VMEM((SEQ, 3 * CH), BF16),
+                pltpu.VMEM((XR, DIM), BF16),
+                pltpu.VMEM((XR, DIM), BF16),
                 pltpu.VMEM((HE, SEQ), BF16),
                 pltpu.SemaphoreType.DMA((N_SEM,)),
                 pltpu.SemaphoreType.DMA((N_SEM,)),

time: 112 us -> 112 us (level)
  no operation moved by 1% of the time
where the time goes in v8:
time: 112 us
  Pallas kernels  111 us (99%)
    pallas_call x1, Pallas kernels, device_step(): pl.pallas_call(step_kernel, out_shape=tuple((pltpu.VMEM(shape, dtype) for...  109 us

profile of v8, /device:TPU:0, one launch (start us, length us, event | category | flops | bytes accessed | tf_op | source)
XLA Modules:
  0.0 111.6 jit_solution(2109715313295112609)
XLA Ops:
  0.6 109.0 %shard_map.101 = (bf16[256,2048]{1,0:T(8,128)(2,1)S(1)}, f32[2048,128]{1,0:T(8,128)S(1)}, f32[256,128]{1,0:T(8,128)S(1)}, f32[256,128]{1,0:T(8,128)S(1)}, f32[512,512]{1,0:T(8,128)S(1)}) custom-call(bf16[1,256,2048]{2,1,0:T(8,128)(2,1)} %x_in.1, bf16[1,256,2048]{2,1,0:T(8,128)(2,1)} %dy_in.1, bf16[8192,128]{1,0:T(8,128)(2,1)} %bitcast.5, ...), custom_call_target="tpu_custom_call" | custom-call | tf_op jit(solution)/shard_map/pallas_call | solution.py:679
  109.7 1.8 %shard_map.102 = (bf16[256,2048]{1,0:T(8,128)(2,1)}, f32[2048,128]{1,0:T(8,128)}, f32[256,128]{1,0:T(8,128)}, f32[256,128]{1,0:T(8,128)}, f32[512,512]{1,0:T(8,128)}) custom-call(bf16[256,2048]{1,0:T(8,128)(2,1)S(1)} %get-tuple-element.15.refs_0_, f32[2048,128]{1,0:T(8,128)S(1)} %get-tuple-element.16.refs_1_, f32[256,128]{1,0:T(8,128)S(1)} %get-tuple-element.17.refs_2_, ...), custom_call_target="tpu_custom_call" | custom-call | tf_op jit(solution)/shard_map/pallas_call | solution.py:725

commit v9 on v8

--- a/solution.py
+++ b/solution.py
@@ -23,24 +23,25 @@
 SC = CH // 2
 WR = 1024
 KC = 256
-NX = 4
+NX = 8
 XR = BLK // NX
 NB = SEQ // BLK
 CAUSAL_ROWS = BLK * NB * (NB + 1) // 2
 
-S_XY, S_XF, S_XC = 0, 4, 8
-S_DY, S_DF, S_DC = 9, 14, 19
-S_KP = 20
-S_PX = 21
-S_PY = 23
-S_XN, S_XNC, S_XNF, S_XNG = 25, 26, 27, 28
-S_A = 29
-S_WO = 33
-S_WQ = 81
-S_KV = 105
-S_XT, S_XU = 117, 121
-N_SEM = 125
-XT = XR // 4
+S_XY, S_XF, S_XC = 0, 8, 16
+S_DY, S_DF, S_DC = 17, 22, 27
+S_KP = 28
+S_PX = 29
+S_PY = 31
+S_XN, S_XNC, S_XNF, S_XNG = 33, 34, 35, 36
+S_A = 37
+S_WO = 41
+S_WQ = 89
+S_KV = 113
+S_XT, S_XU = 125, 127
+N_SEM = 129
+NT = 2
+XT = XR // NT
 VMEM_LIMIT = 63 * 2 ** 20 - 3328 * 1024
 
 
@@ -157,7 +158,7 @@
 
     @pl.when(inner == 0)
     def _():
-        for j in range(4):
+        for j in range(NT):
             xt_edge(j).start()
         xn_edge(m).start()
         for i in range(1, NX - 1):
@@ -191,7 +192,7 @@
 
     @pl.when(inner == 1)
     def _():
-        for j in range(4):
+        for j in range(NT):
             xt_edge(j).wait_recv()
             xt_far(j).start()
         for i in range(1, NX):
@@ -215,7 +216,7 @@
 
     @pl.when(inner == 1)
     def _():
-        for j in range(4):
+        for j in range(NT):
             xt_far(j).wait_recv()
         xt_back().start()
 
@@ -251,6 +252,12 @@
 
     def half_col(s):
         return pl.ds(s * SC, SC)
+
+    def wo_pass(k, h):
+        for s in range(2):
+            wo_edge(k, s, h).wait_recv()
+            so[k, s, h] = (pw[k, head_rows(h), half_col(s)] + ro[k, s, h].astype(F32)).astype(BF16)
+            wo_swap(k, s, h).start()
 
     def wo_first(s, h):
         v = nn(ot[pl.ds(h * HD, HD), :], dyg[:, dcol(s)])
@@ -324,11 +331,9 @@
         for s in range(2):
             wo_first(s, h)
 
-    def wo_pass(k, h):
-        for s in range(2):
-            wo_edge(k, s, h).wait_recv()
-            so[k, s, h] = (pw[k, head_rows(h), half_col(s)] + ro[k, s, h].astype(F32)).astype(BF16)
-            wo_swap(k, s, h).start()
+        @pl.when(inner == 1)
+        def _(h=h):
+            wo_pass(0, h - 2)
 
     def wo_return(h):
         for s in range(2):
@@ -354,8 +359,7 @@
 
             @pl.when(inner == 1)
             def _(i=i):
-                for h in (2 * i - 2, 2 * i - 1):
-                    wo_pass(0, h)
+                wo_pass(0, i + 1)
 
     def a_copy(h):
         r = head_rows(h)
@@ -620,7 +624,7 @@
     dy_core(m).wait_send()
     @pl.when(inner == 0)
     def _():
-        for j in range(4):
+        for j in range(NT):
             xt_edge(j).wait_send()
         xn_edge(m).wait_send()
         for h in range(NH):
@@ -635,7 +639,7 @@
     @pl.when(inner == 1)
     def _():
         x_far(NX - 1, m).wait_send()
-        for j in range(4):
+        for j in range(NT):
             xt_far(j).wait_send()
         xt_back().wait_send()
         xn_send(m, S_XNF, far_dev).wait_send()

time: 112 us -> 111 us (level)
  Pallas kernels: 111 us -> 109 us
    pallas_call x1, Pallas kernels: 109 us -> 108 us  [device_step(): pl.pallas_call(step_kernel, out_shape=tuple((pltpu.VMEM(shape, dtype) for...]
where the time goes in v9:
time: 111 us; the launch traced here: 110 us
  Pallas kernels  109 us (98%)
    pallas_call x1, Pallas kernels, device_step(): pl.pallas_call(step_kernel, out_shape=tuple((pltpu.VMEM(shape, dtype) for...  108 us

profile of v9, /device:TPU:0, one launch (start us, length us, event | category | flops | bytes accessed | tf_op | source)
XLA Modules:
  0.0 110.3 jit_solution(5713019990310292541)
XLA Ops:
  0.6 107.7 %shard_map.101 = (bf16[256,2048]{1,0:T(8,128)(2,1)S(1)}, f32[2048,128]{1,0:T(8,128)S(1)}, f32[256,128]{1,0:T(8,128)S(1)}, f32[256,128]{1,0:T(8,128)S(1)}, f32[512,512]{1,0:T(8,128)S(1)}) custom-call(bf16[1,256,2048]{2,1,0:T(8,128)(2,1)} %x_in.1, bf16[1,256,2048]{2,1,0:T(8,128)(2,1)} %dy_in.1, bf16[8192,128]{1,0:T(8,128)(2,1)} %bitcast.5, ...), custom_call_target="tpu_custom_call" | custom-call | tf_op jit(solution)/shard_map/pallas_call | solution.py:683
  108.3 1.8 %shard_map.102 = (bf16[256,2048]{1,0:T(8,128)(2,1)}, f32[2048,128]{1,0:T(8,128)}, f32[256,128]{1,0:T(8,128)}, f32[256,128]{1,0:T(8,128)}, f32[512,512]{1,0:T(8,128)}) custom-call(bf16[256,2048]{1,0:T(8,128)(2,1)S(1)} %get-tuple-element.15.refs_0_, f32[2048,128]{1,0:T(8,128)S(1)} %get-tuple-element.16.refs_1_, f32[256,128]{1,0:T(8,128)S(1)} %get-tuple-element.17.refs_2_, ...), custom_call_target="tpu_custom_call" | custom-call | tf_op jit(solution)/shard_map/pallas_call | solution.py:729

commit v10 on v7

--- a/solution.py
+++ b/solution.py
@@ -23,22 +23,22 @@
 SC = CH // 2
 WR = 1024
 KC = 256
-NX = 4
+NX = 8
 XR = BLK // NX
 NB = SEQ // BLK
 CAUSAL_ROWS = BLK * NB * (NB + 1) // 2
 
-S_XY, S_XF, S_XC = 0, 4, 8
-S_DY, S_DF, S_DC = 9, 14, 19
-S_KP = 20
-S_PX = 21
-S_PY = 23
-S_XN, S_XNC, S_XNF, S_XNG = 25, 26, 27, 28
-S_A = 29
-S_WO = 33
-S_WQ = 81
-S_KV = 105
-N_SEM = 117
+S_XY, S_XF, S_XC = 0, 8, 16
+S_DY, S_DF, S_DC = 17, 22, 27
+S_KP = 28
+S_PX = 29
+S_PY = 31
+S_XN, S_XNC, S_XNF, S_XNG = 33, 36, 37, 40
+S_A = 43
+S_WO = 47
+S_WQ = 95
+S_KV = 119
+N_SEM = 131
 VMEM_LIMIT = 63 * 2 ** 20 - 3328 * 1024
 
 
@@ -135,11 +135,24 @@
     def dy_core(block):
         return remote(dyg.at[rows(block)], dyg.at[rows(block)], S_DC, core_dev)
 
-    def xn_edge(block):
-        return remote(xg.at[rows(block), pl.ds(pl.multiple_of(x_off, CH), 3 * CH)], xn.at[rows(block)], S_XN, pair_dev)
-
-    def xn_send(block, sem, dev):
-        return remote(xn.at[rows(block)], xn.at[rows(block)], sem, dev)
+    def ncol(k):
+        return pl.ds(pl.multiple_of(chunk(k) * CH - x_off, CH), CH)
+
+    def xn_edge(k):
+        return remote(xg.at[rows(m), col(k)], xn.at[rows(m), ncol(k)], S_XN + k, pair_dev)
+
+    def xn_core(block):
+        return remote(xn.at[rows(block)], xn.at[rows(block)], S_XNC, core_dev)
+
+    def xn_far(k, block):
+        return remote(xn.at[rows(block), ncol(k)], xn.at[rows(block), ncol(k)], S_XNF + k, far_dev)
+
+    def xn_fwd(k, block):
+        return remote(xn.at[rows(block), ncol(k)], xn.at[rows(block), ncol(k)], S_XNG + k, core_dev)
+
+    def take_xn(k):
+        xn_far(k, far_m).wait_recv()
+        xn_fwd(k, far_m).start()
 
     loads[0].wait()
     for i in range(NX):
@@ -147,7 +160,8 @@
 
     @pl.when(inner == 0)
     def _():
-        xn_edge(m).start()
+        for k in range(3):
+            xn_edge(k).start()
 
     x_core(m).start()
     loads[1].wait()
@@ -218,6 +232,12 @@
     def half_col(s):
         return pl.ds(s * SC, SC)
 
+    def wo_pass(k, h):
+        for s in range(2):
+            wo_edge(k, s, h).wait_recv()
+            so[k, s, h] = (pw[k, head_rows(h), half_col(s)] + ro[k, s, h].astype(F32)).astype(BF16)
+            wo_swap(k, s, h).start()
+
     def wo_first(s, h):
         v = nn(ot[pl.ds(h * HD, HD), :], dyg[:, dcol(s)])
 
@@ -232,9 +252,10 @@
 
     @pl.when(inner == 1)
     def _():
-        xn_edge(m).wait_recv()
-        xn_send(m, S_XNF, far_dev).start()
-        xn_send(m, S_XNC, core_dev).start()
+        for k in range(3):
+            xn_edge(k).wait_recv()
+            xn_far(k, m).start()
+        xn_core(m).start()
 
     scale = HD ** -0.5
     exp_scale = scale * math.log2(math.e)
@@ -274,12 +295,13 @@
     fwd_head(0, 3, NB)
     dy_fwd(0, diag_m).wait_recv()
     wo_first(0, 0)
-    fwd_head(1, 0, 3)
+    fwd_head(1, 0, 2)
     take_dy(1)
+    fwd_head(1, 2, 3)
+    dy_fwd(1, diag_m).wait_recv()
+    wo_first(1, 0)
     fwd_head(1, 3, NB)
     wo_first(0, 1)
-    dy_fwd(1, diag_m).wait_recv()
-    wo_first(1, 0)
     wo_first(1, 1)
     for h in range(2, NH):
         fwd_head(h, 0, 3)
@@ -289,11 +311,9 @@
         for s in range(2):
             wo_first(s, h)
 
-    def wo_pass(k, h):
-        for s in range(2):
-            wo_edge(k, s, h).wait_recv()
-            so[k, s, h] = (pw[k, head_rows(h), half_col(s)] + ro[k, s, h].astype(F32)).astype(BF16)
-            wo_swap(k, s, h).start()
+        @pl.when(inner == 1)
+        def _(h=h):
+            wo_pass(0, h - 2)
 
     def wo_return(h):
         for s in range(2):
@@ -313,14 +333,14 @@
         dy_fwd(i + 1, diag_m).wait_recv()
         pw[i] = nn(ot[...], dyg[:, col(i)])
         if i < 3:
-            @pl.when(inner == 0)
-            def _(i=i):
-                wo_send(i)
+            if i == 1:
+                @pl.when(inner == 0)
+                def _():
+                    wo_send(1)
 
             @pl.when(inner == 1)
             def _(i=i):
-                for h in (2 * i - 2, 2 * i - 1):
-                    wo_pass(0, h)
+                wo_pass(0, i + 1)
 
     def a_copy(h):
         r = head_rows(h)
@@ -331,9 +351,6 @@
 
     def wq_back(s, h):
         return remote(sq.at[2, s, h], rq.at[2, s, h], S_WQ + 16 + s * 4 + h, pair_dev)
-
-    def ncol(k):
-        return pl.ds(pl.multiple_of(chunk(k) * CH - x_off, CH), CH)
 
     def spot(k, s, h=0, n=1):
         return prob.at[1 + k // 2, pl.ds(((k % 2) * 2 + s) * HE + h * HD, n * HD)]
@@ -396,6 +413,11 @@
             wo_pass(1, h)
             wo_return(h)
 
+            for at_h, piece in ((1, 0), (3, 1)):
+                @pl.when(h == at_h)
+                def _(piece=piece):
+                    take_xn(piece)
+
         return carry
 
     lax.fori_loop(0, NH, bwd_head, 0)
@@ -478,12 +500,16 @@
             for t in range(2):
                 kv_part(skv, k, t)[...] = kv_own(k, t).astype(BF16)
                 kv_edge(k, t).start()
+        wo_send(2)
     @pl.when(inner == 1)
     def _():
-        xn_send(far_m, S_XNF, far_dev).wait_recv()
-        xn_send(far_m, S_XNG, core_dev).start()
         wq_own(0, chunk(0))
+        xn_core(core_m).wait_recv()
+        xn_fwd(0, diag_m).wait_recv()
+        combine(0, (0,))
         wq_own(1, chunk(1))
+        xn_fwd(1, diag_m).wait_recv()
+        combine(0, (1,))
 
     dx_part(far_m, put_own)
     px_copy(0).wait_recv()
@@ -497,12 +523,12 @@
 
     @pl.when(inner == 1)
     def _():
-        xn_send(core_m, S_XNC, core_dev).wait_recv()
-        xn_send(diag_m, S_XNG, core_dev).wait_recv()
-        combine(0)
+        combine(1)
+        take_xn(2)
         wq_own(3, chunk(3))
-        combine(1)
         outer(0)
+        combine(2)
+        outer(1)
 
     dx_part(core_m, put_sx(1))
     px_copy(1).start()
@@ -511,26 +537,20 @@
 
     @pl.when(inner == 1)
     def _():
-        combine(2)
-        outer(1)
         combine(3, (0,))
         outer(2)
+        kv_pass(0)
+        combine(3, (1,))
+        xn_fwd(2, diag_m).wait_recv()
         v = nn(abuf[...], xn[:, ncol(2)])
         for s in range(2):
             spot(2, s, 0, NH)[...] += v[:, s * SC:(s + 1) * SC]
-        kv_pass(0)
-        combine(3, (1,))
+        kv_pass(1)
         outer(3)
-        kv_pass(1)
         for t in range(2):
             kv_swap(0, t).wait_recv()
             kv_part(skv, 2, t)[...] = (kv_own(3, t) + kv_part(rkv, 3, t)[...].astype(F32)).astype(BF16)
             kv_back(t).start()
-        for h in range(NH):
-            for s in range(2):
-                wo_edge(2, s, h).wait_recv()
-                wo_swap(1, s, h).wait_recv()
-                woo[head_rows(h), half_col(s)] = pw[2, head_rows(h), half_col(s)] + ro[2, s, h].astype(F32) + ro[4, s, h].astype(F32)
 
     @pl.when(inner == 0)
     def _():
@@ -563,6 +583,11 @@
             kv_edge(2, t).wait_recv()
             kv_swap(1, t).wait_recv()
             kv_out[t][...] = (kv_own(2, t) + kv_part(rkv, 2, t)[...].astype(F32) + kv_part(rkv, 4, t)[...].astype(F32)).T
+        for h in range(NH):
+            for s in range(2):
+                wo_edge(2, s, h).wait_recv()
+                wo_swap(1, s, h).wait_recv()
+                woo[head_rows(h), half_col(s)] = pw[2, head_rows(h), half_col(s)] + ro[2, s, h].astype(F32) + ro[4, s, h].astype(F32)
 
     @pl.when(inner == 0)
     def _():
@@ -584,7 +609,8 @@
     dy_core(m).wait_send()
     @pl.when(inner == 0)
     def _():
-        xn_edge(m).wait_send()
+        for k in range(3):
+            xn_edge(k).wait_send()
         for h in range(NH):
             a_copy(h).wait_send()
         for k in range(3):
@@ -596,9 +622,10 @@
 
     @pl.when(inner == 1)
     def _():
-        xn_send(m, S_XNF, far_dev).wait_send()
-        xn_send(m, S_XNC, core_dev).wait_send()
-        xn_send(far_m, S_XNG, core_dev).wait_send()
+        xn_core(m).wait_send()
+        for k in range(3):
+            xn_far(k, m).wait_send()
+            xn_fwd(k, far_m).wait_send()
         for t in range(2):
             for k in range(2):
                 kv_swap(k, t).wait_send()

time: 112 us -> 105 us (0.938)
  Pallas kernels: 111 us -> 104 us
    pallas_call x1, Pallas kernels: 109 us -> 102 us  [device_step(): pl.pallas_call(step_kernel, out_shape=tuple((pltpu.VMEM(shape, dtype) for...]
where the time goes in v10:
time: 105 us; the launch traced here: 104 us
  Pallas kernels  104 us (99%)
    pallas_call x1, Pallas kernels, device_step(): pl.pallas_call(step_kernel, out_shape=tuple((pltpu.VMEM(shape, dtype) for...  102 us

profile of v10, /device:TPU:0, one launch (start us, length us, event | category | flops | bytes accessed | tf_op | source)
XLA Modules:
  0.0 104.4 jit_solution(16530622527264801943)
XLA Ops:
  0.6 101.8 %shard_map.101 = (bf16[256,2048]{1,0:T(8,128)(2,1)S(1)}, f32[2048,128]{1,0:T(8,128)S(1)}, f32[256,128]{1,0:T(8,128)S(1)}, f32[256,128]{1,0:T(8,128)S(1)}, f32[512,512]{1,0:T(8,128)S(1)}) custom-call(bf16[1,256,2048]{2,1,0:T(8,128)(2,1)} %x_in.1, bf16[1,256,2048]{2,1,0:T(8,128)(2,1)} %dy_in.1, bf16[8192,128]{1,0:T(8,128)(2,1)} %bitcast.5, ...), custom_call_target="tpu_custom_call" | custom-call | tf_op jit(solution)/shard_map/pallas_call | solution.py:664
  102.4 1.8 %shard_map.102 = (bf16[256,2048]{1,0:T(8,128)(2,1)}, f32[2048,128]{1,0:T(8,128)}, f32[256,128]{1,0:T(8,128)}, f32[256,128]{1,0:T(8,128)}, f32[512,512]{1,0:T(8,128)}) custom-call(bf16[256,2048]{1,0:T(8,128)(2,1)S(1)} %get-tuple-element.15.refs_0_, f32[2048,128]{1,0:T(8,128)S(1)} %get-tuple-element.16.refs_1_, f32[256,128]{1,0:T(8,128)S(1)} %get-tuple-element.17.refs_2_, ...), custom_call_target="tpu_custom_call" | custom-call | tf_op jit(solution)/shard_map/pallas_call | solution.py:708

commit v11 on v10

--- a/solution.py
+++ b/solution.py
@@ -38,7 +38,10 @@
 S_WO = 47
 S_WQ = 95
 S_KV = 119
-N_SEM = 131
+S_XT, S_XU = 131, 133
+N_SEM = 135
+NT = 2
+XT = XR // NT
 VMEM_LIMIT = 63 * 2 ** 20 - 3328 * 1024
 
 
@@ -52,7 +55,7 @@
 
 def step_kernel(x_in, dy_in, wq_in, wk_in, wv_in, wo_in, dxo, wqo, dko, dvo, woo,
                 xg, dyg, wq8, wst, wqkv, wo, qkv, kt, vt, prob, pbuf, ot, dout, at, am, dkv, pw, pkv,
-                kvs, kvr, so, ro, sq, rq, skv, rkv, sx, rx, sy, ry, xn, abuf, ssem, rsem, lsem):
+                kvs, kvr, so, ro, sq, rq, skv, rkv, sx, rx, sy, ry, xn, xta, xtb, abuf, ssem, rsem, lsem):
     pod = lax.axis_index("pod")
     z = lax.axis_index("data")
     m = lax.axis_index("model")
@@ -154,19 +157,36 @@
         xn_far(k, far_m).wait_recv()
         xn_fwd(k, far_m).start()
 
+    def xt_edge(j):
+        return remote(xg.at[rows(m, XT, (NX - 1) * XR + j * XT)], xta.at[pl.ds(j * XT, XT)], S_XT + j, pair_dev)
+
+    def xt_far(j):
+        return remote(xta.at[pl.ds(j * XT, XT)], xtb.at[pl.ds(j * XT, XT)], S_XU + j, far_dev)
+
+    def xt_back():
+        return remote(xtb, xg.at[rows(far_m, XR, (NX - 1) * XR)], S_XY + NX - 1, pair_dev)
+
     loads[0].wait()
-    for i in range(NX):
+    for i in range(2):
         x_far(i, m).start()
 
     @pl.when(inner == 0)
     def _():
+        for j in range(NT):
+            xt_edge(j).start()
         for k in range(3):
             xn_edge(k).start()
+        for i in range(2, NX - 1):
+            x_far(i, m).start()
 
     x_core(m).start()
     loads[1].wait()
-    for i in range(5):
-        dy_far(i, m).start()
+
+    @pl.when(inner == 0)
+    def _():
+        for i in range(5):
+            dy_far(i, m).start()
+
     dy_core(m).start()
     for ld in loads[2:]:
         ld.wait()
@@ -184,6 +204,16 @@
         return carry
 
     lax.fori_loop(0, DIM * NH // WR, wq_block, 0)
+
+    @pl.when(inner == 1)
+    def _():
+        for j in range(NT):
+            xt_edge(j).wait_recv()
+            xt_far(j).start()
+        for i in range(2, NX):
+            x_far(i, m).start()
+        for i in range(5):
+            dy_far(i, m).start()
 
     def project(r):
         qkv[r, :] = nn(xg[r, :], wqkv[...]).astype(BF16)
@@ -199,7 +229,14 @@
     flip(m)
     flip(core_m)
 
-    def x_piece(i, carry):
+    @pl.when(inner == 1)
+    def _():
+        for j in range(NT):
+            xt_far(j).wait_recv()
+        xt_back().start()
+
+    def x_piece(step, carry):
+        i = step + (1 - inner) * (step // (NX - 2)) * (1 - 2 * (step % 2))
         x_far(i, far_m).wait_recv()
         x_fwd(i, far_m).start()
         project(rows(far_m, XR, i * XR))
@@ -413,14 +450,21 @@
             wo_pass(1, h)
             wo_return(h)
 
-            for at_h, piece in ((1, 0), (3, 1)):
-                @pl.when(h == at_h)
-                def _(piece=piece):
-                    take_xn(piece)
+            @pl.when(h == 2)
+            def _():
+                take_xn(0)
 
         return carry
 
     lax.fori_loop(0, NH, bwd_head, 0)
+
+    @pl.when(inner == 1)
+    def _():
+        take_xn(1)
+        wq_own(0, chunk(0))
+        xn_core(core_m).wait_recv()
+        xn_fwd(0, diag_m).wait_recv()
+        combine(0, (0,))
 
     dkb = (dkv[:, pl.ds(0, HD)] * scale).astype(BF16)
     dvb = dkv[:, pl.ds(HD, HD)].astype(BF16)
@@ -503,10 +547,6 @@
         wo_send(2)
     @pl.when(inner == 1)
     def _():
-        wq_own(0, chunk(0))
-        xn_core(core_m).wait_recv()
-        xn_fwd(0, diag_m).wait_recv()
-        combine(0, (0,))
         wq_own(1, chunk(1))
         xn_fwd(1, diag_m).wait_recv()
         combine(0, (1,))
@@ -599,8 +639,9 @@
             kv_back(t).wait_recv()
             kv_out[t][...] = (kv_own(3, t) + kv_part(rkv, 3, t)[...].astype(F32)).T
 
+    for i in range(NX - 1):
+        x_far(i, m).wait_send()
     for i in range(NX):
-        x_far(i, m).wait_send()
         x_fwd(i, far_m).wait_send()
     x_core(m).wait_send()
     for i in range(5):
@@ -609,6 +650,8 @@
     dy_core(m).wait_send()
     @pl.when(inner == 0)
     def _():
+        for j in range(NT):
+            xt_edge(j).wait_send()
         for k in range(3):
             xn_edge(k).wait_send()
         for h in range(NH):
@@ -622,6 +665,10 @@
 
     @pl.when(inner == 1)
     def _():
+        x_far(NX - 1, m).wait_send()
+        for j in range(NT):
+            xt_far(j).wait_send()
+        xt_back().wait_send()
         xn_core(m).wait_send()
         for k in range(3):
             xn_far(k, m).wait_send()
@@ -698,6 +745,8 @@
                 pltpu.VMEM((BLK, DIM), BF16),
                 pltpu.VMEM((BLK, DIM), BF16),
                 pltpu.VMEM((SEQ, 3 * CH), BF16),
+                pltpu.VMEM((XR, DIM), BF16),
+                pltpu.VMEM((XR, DIM), BF16),
                 pltpu.VMEM((HE, SEQ), BF16),
                 pltpu.SemaphoreType.DMA((N_SEM,)),
                 pltpu.SemaphoreType.DMA((N_SEM,)),

time: 105 us -> 107 us (1.019)
    pallas_call x1, Pallas kernels: 102 us -> 103 us  [device_step(): pl.pallas_call(step_kernel, out_shape=tuple((pltpu.VMEM(shape, dtype) for...]
where the time goes in v11:
time: 107 us; the launch traced here: 106 us
  Pallas kernels  105 us (98%)
    pallas_call x1, Pallas kernels, device_step(): pl.pallas_call(step_kernel, out_shape=tuple((pltpu.VMEM(shape, dtype) for...  103 us

profile of v11, /device:TPU:0, one launch (start us, length us, event | category | flops | bytes accessed | tf_op | source)
XLA Modules:
  0.0 105.5 jit_solution(12226006419933844024)
XLA Ops:
  0.6 102.9 %shard_map.101 = (bf16[256,2048]{1,0:T(8,128)(2,1)S(1)}, f32[2048,128]{1,0:T(8,128)S(1)}, f32[256,128]{1,0:T(8,128)S(1)}, f32[256,128]{1,0:T(8,128)S(1)}, f32[512,512]{1,0:T(8,128)S(1)}) custom-call(bf16[1,256,2048]{2,1,0:T(8,128)(2,1)} %x_in.1, bf16[1,256,2048]{2,1,0:T(8,128)(2,1)} %dy_in.1, bf16[8192,128]{1,0:T(8,128)(2,1)} %bitcast.5, ...), custom_call_target="tpu_custom_call" | custom-call | tf_op jit(solution)/shard_map/pallas_call | solution.py:711
  103.6 1.8 %shard_map.102 = (bf16[256,2048]{1,0:T(8,128)(2,1)}, f32[2048,128]{1,0:T(8,128)}, f32[256,128]{1,0:T(8,128)}, f32[256,128]{1,0:T(8,128)}, f32[512,512]{1,0:T(8,128)}) custom-call(bf16[256,2048]{1,0:T(8,128)(2,1)S(1)} %get-tuple-element.15.refs_0_, f32[2048,128]{1,0:T(8,128)S(1)} %get-tuple-element.16.refs_1_, f32[256,128]{1,0:T(8,128)S(1)} %get-tuple-element.17.refs_2_, ...), custom_call_target="tpu_custom_call" | custom-call | tf_op jit(solution)/shard_map/pallas_call | solution.py:757

commit v12 on v11

--- a/solution.py
+++ b/solution.py
@@ -465,6 +465,7 @@
         xn_core(core_m).wait_recv()
         xn_fwd(0, diag_m).wait_recv()
         combine(0, (0,))
+        combine(1, (0,))
 
     dkb = (dkv[:, pl.ds(0, HD)] * scale).astype(BF16)
     dvb = dkv[:, pl.ds(HD, HD)].astype(BF16)
@@ -529,28 +530,8 @@
             kv_part(skv, k, t)[...] = (kv_own(k, t) + kv_part(rkv, k, t)[...].astype(F32)).astype(BF16)
             kv_swap(k, t).start()
 
-    kvs[...] = kv_half(1 - c).astype(BF16)
-    kp_copy = remote(kvs, kvr, S_KP, core_dev)
-    kp_copy.start()
     dx_part(diag_m, put_sx(0))
     px_copy(0).start()
-    pkv[...] = kv_half(c)
-    kp_copy.wait_recv()
-    pkv[...] += kvr[...].astype(F32)
-
-    @pl.when(inner == 0)
-    def _():
-        for k in range(3):
-            for t in range(2):
-                kv_part(skv, k, t)[...] = kv_own(k, t).astype(BF16)
-                kv_edge(k, t).start()
-        wo_send(2)
-    @pl.when(inner == 1)
-    def _():
-        wq_own(1, chunk(1))
-        xn_fwd(1, diag_m).wait_recv()
-        combine(0, (1,))
-
     dx_part(far_m, put_own)
     px_copy(0).wait_recv()
     for i in range(2):
@@ -563,11 +544,31 @@
 
     @pl.when(inner == 1)
     def _():
-        combine(1)
+        wq_own(1, chunk(1))
+        xn_fwd(1, diag_m).wait_recv()
+        combine(0, (1,))
+        combine(1, (1,))
+
+    kvs[...] = kv_half(1 - c).astype(BF16)
+    kp_copy = remote(kvs, kvr, S_KP, core_dev)
+    kp_copy.start()
+    pkv[...] = kv_half(c)
+    kp_copy.wait_recv()
+    pkv[...] += kvr[...].astype(F32)
+
+    @pl.when(inner == 0)
+    def _():
+        for k in range(3):
+            for t in range(2):
+                kv_part(skv, k, t)[...] = kv_own(k, t).astype(BF16)
+                kv_edge(k, t).start()
+        wo_send(2)
+    @pl.when(inner == 1)
+    def _():
+        combine(2)
         take_xn(2)
         wq_own(3, chunk(3))
         outer(0)
-        combine(2)
         outer(1)
 
     dx_part(core_m, put_sx(1))

time: 107 us -> 107 us (level)
  no operation moved by 1% of the time
where the time goes in v12:
time: 107 us; the launch traced here: 106 us
  Pallas kernels  105 us (98%)
    pallas_call x1, Pallas kernels, device_step(): pl.pallas_call(step_kernel, out_shape=tuple((pltpu.VMEM(shape, dtype) for...  103 us

profile of v12, /device:TPU:0, one launch (start us, length us, event | category | flops | bytes accessed | tf_op | source)
XLA Modules:
  0.0 105.5 jit_solution(6406370133254720938)
XLA Ops:
  0.6 102.9 %shard_map.101 = (bf16[256,2048]{1,0:T(8,128)(2,1)S(1)}, f32[2048,128]{1,0:T(8,128)S(1)}, f32[256,128]{1,0:T(8,128)S(1)}, f32[256,128]{1,0:T(8,128)S(1)}, f32[512,512]{1,0:T(8,128)S(1)}) custom-call(bf16[1,256,2048]{2,1,0:T(8,128)(2,1)} %x_in.1, bf16[1,256,2048]{2,1,0:T(8,128)(2,1)} %dy_in.1, bf16[8192,128]{1,0:T(8,128)(2,1)} %bitcast.5, ...), custom_call_target="tpu_custom_call" | custom-call | tf_op jit(solution)/shard_map/pallas_call | solution.py:712
  103.6 1.8 %shard_map.102 = (bf16[256,2048]{1,0:T(8,128)(2,1)}, f32[2048,128]{1,0:T(8,128)}, f32[256,128]{1,0:T(8,128)}, f32[256,128]{1,0:T(8,128)}, f32[512,512]{1,0:T(8,128)}) custom-call(bf16[256,2048]{1,0:T(8,128)(2,1)S(1)} %get-tuple-element.15.refs_0_, f32[2048,128]{1,0:T(8,128)S(1)} %get-tuple-element.16.refs_1_, f32[256,128]{1,0:T(8,128)S(1)} %get-tuple-element.17.refs_2_, ...), custom_call_target="tpu_custom_call" | custom-call | tf_op jit(solution)/shard_map/pallas_call | solution.py:758

commit v13 on v12

--- a/solution.py
+++ b/solution.py
@@ -38,10 +38,10 @@
 S_WO = 47
 S_WQ = 95
 S_KV = 119
-S_XT, S_XU = 131, 133
-N_SEM = 135
-NT = 2
-XT = XR // NT
+S_XT, S_XU, S_XV = 131, 132, 133
+N_SEM = 134
+NT = 1
+XT = XR // 2
 VMEM_LIMIT = 63 * 2 ** 20 - 3328 * 1024
 
 
@@ -158,13 +158,17 @@
         xn_fwd(k, far_m).start()
 
     def xt_edge(j):
-        return remote(xg.at[rows(m, XT, (NX - 1) * XR + j * XT)], xta.at[pl.ds(j * XT, XT)], S_XT + j, pair_dev)
+        return remote(xg.at[rows(m, XT, (NX - 1) * XR + XT)], xta.at[pl.ds(j * XT, XT)], S_XT + j, pair_dev)
 
     def xt_far(j):
         return remote(xta.at[pl.ds(j * XT, XT)], xtb.at[pl.ds(j * XT, XT)], S_XU + j, far_dev)
 
     def xt_back():
-        return remote(xtb, xg.at[rows(far_m, XR, (NX - 1) * XR)], S_XY + NX - 1, pair_dev)
+        return remote(xtb, xg.at[rows(far_m, XT, (NX - 1) * XR + XT)], S_XV, pair_dev)
+
+    def x_last(block):
+        r = rows(block, XT, (NX - 1) * XR)
+        return remote(xg.at[r], xg.at[r], S_XY + NX - 1, far_dev)
 
     loads[0].wait()
     for i in range(2):
@@ -178,6 +182,7 @@
             xn_edge(k).start()
         for i in range(2, NX - 1):
             x_far(i, m).start()
+        x_last(m).start()
 
     x_core(m).start()
     loads[1].wait()
@@ -235,9 +240,18 @@
             xt_far(j).wait_recv()
         xt_back().start()
 
-    def x_piece(step, carry):
-        i = step + (1 - inner) * (step // (NX - 2)) * (1 - 2 * (step % 2))
-        x_far(i, far_m).wait_recv()
+    def x_piece(i, carry):
+        split = (1 - inner) * (i // (NX - 1))
+
+        @pl.when(split == 0)
+        def _():
+            x_far(i, far_m).wait_recv()
+
+        @pl.when(split == 1)
+        def _():
+            x_last(far_m).wait_recv()
+            xt_back().wait_recv()
+
         x_fwd(i, far_m).start()
         project(rows(far_m, XR, i * XR))
         x_fwd(i, diag_m).wait_recv()
@@ -651,6 +665,7 @@
     dy_core(m).wait_send()
     @pl.when(inner == 0)
     def _():
+        x_last(m).wait_send()
         for j in range(NT):
             xt_edge(j).wait_send()
         for k in range(3):
@@ -746,8 +761,8 @@
                 pltpu.VMEM((BLK, DIM), BF16),
                 pltpu.VMEM((BLK, DIM), BF16),
                 pltpu.VMEM((SEQ, 3 * CH), BF16),
-                pltpu.VMEM((XR, DIM), BF16),
-                pltpu.VMEM((XR, DIM), BF16),
+                pltpu.VMEM((XT, DIM), BF16),
+                pltpu.VMEM((XT, DIM), BF16),
                 pltpu.VMEM((HE, SEQ), BF16),
                 pltpu.SemaphoreType.DMA((N_SEM,)),
                 pltpu.SemaphoreType.DMA((N_SEM,)),

time: 107 us -> 105 us (0.981); the launches traced: 106 us -> 105 us
  no operation moved by 1% of the time
where the time goes in v13:
time: 105 us
  Pallas kernels  104 us (99%)
    pallas_call x1, Pallas kernels, device_step(): pl.pallas_call(step_kernel, out_shape=tuple((pltpu.VMEM(shape, dtype) for...  102 us

profile of v13, /device:TPU:0, one launch (start us, length us, event | category | flops | bytes accessed | tf_op | source)
XLA Modules:
  0.0 104.7 jit_solution(10685675000557918430)
XLA Ops:
  0.6 102.1 %shard_map.101 = (bf16[256,2048]{1,0:T(8,128)(2,1)S(1)}, f32[2048,128]{1,0:T(8,128)S(1)}, f32[256,128]{1,0:T(8,128)S(1)}, f32[256,128]{1,0:T(8,128)S(1)}, f32[512,512]{1,0:T(8,128)S(1)}) custom-call(bf16[1,256,2048]{2,1,0:T(8,128)(2,1)} %x_in.1, bf16[1,256,2048]{2,1,0:T(8,128)(2,1)} %dy_in.1, bf16[8192,128]{1,0:T(8,128)(2,1)} %bitcast.5, ...), custom_call_target="tpu_custom_call" | custom-call | tf_op jit(solution)/shard_map/pallas_call | solution.py:727
  102.8 1.8 %shard_map.102 = (bf16[256,2048]{1,0:T(8,128)(2,1)}, f32[2048,128]{1,0:T(8,128)}, f32[256,128]{1,0:T(8,128)}, f32[256,128]{1,0:T(8,128)}, f32[512,512]{1,0:T(8,128)}) custom-call(bf16[256,2048]{1,0:T(8,128)(2,1)S(1)} %get-tuple-element.15.refs_0_, f32[2048,128]{1,0:T(8,128)S(1)} %get-tuple-element.16.refs_1_, f32[256,128]{1,0:T(8,128)S(1)} %get-tuple-element.17.refs_2_, ...), custom_call_target="tpu_custom_call" | custom-call | tf_op jit(solution)/shard_map/pallas_call | solution.py:773
